TPU v7x, 16 devices: a whole 2x2x2 slice. The times are simulated.
16 devices in a mesh: fsdp: 16 (over z, y, x, core).
Axes of the slice: x: 2, y: 2, z: 2, core: 2. Of those that a mesh axis runs over, the one named last changes fastest.
Arguments:
- tokens: int32 [32, 512], P('fsdp')
- positions: int32 [32, 512], P('fsdp')
- embed_table: bfloat16 [152064, 1024], P('fsdp')
- attn_norm: bfloat16 [1024], P('fsdp')
- w_query: bfloat16 [1024, 2048], P('fsdp')
- w_key: bfloat16 [1024, 1024], P('fsdp')
- w_value: bfloat16 [1024, 1024], P('fsdp')
- q_norm: bfloat16 [128], replicated
- k_norm: bfloat16 [128], replicated
- w_out: bfloat16 [2048, 1024], P('fsdp')
- mlp_norm: bfloat16 [1024], P('fsdp')
- w_gate: bfloat16 [1024, 3072], P('fsdp')
- w_up: bfloat16 [1024, 3072], P('fsdp')
- w_down: bfloat16 [3072, 1024], P('fsdp')
- dy_out: bfloat16 [32, 512, 1024], P('fsdp')
Outputs:
- output 1: bfloat16 [32, 512, 1024], P('fsdp')
- output 2: float32 [152064, 1024], P('fsdp')
- output 3: float32 [1024], P('fsdp')
- output 4: float32 [1024, 2048], P('fsdp')
- output 5: float32 [1024, 1024], P('fsdp')
- output 6: float32 [1024, 1024], P('fsdp')
- output 7: float32 [128], replicated
- output 8: float32 [128], replicated
- output 9: float32 [2048, 1024], P('fsdp')
- output 10: float32 [1024], P('fsdp')
- output 11: float32 [1024, 3072], P('fsdp')
- output 12: float32 [1024, 3072], P('fsdp')
- output 13: float32 [3072, 1024], P('fsdp')
All inputs are finite; a program needn't handle non-finite values.
Results may differ from a plain program's by a relative error of at most 0.0158748.
Values are sent between devices in bfloat16 or wider.
A program may use at most 1 GiB of HBM per device.

v0:
```python
import math
import jax
import jax.numpy as jnp
from jax import lax
from jax.sharding import PartitionSpec as P

NORM_EPS = 1e-6
ROPE_THETA = 1.0e6
AXIS_NAME = 'fsdp'
SHARDED = (True, True, True, True, False, False, True, True, True, True, True)


def rope_tables(positions, head_dim):
    half_dim = head_dim // 2
    inv_freq = jnp.exp(jnp.arange(half_dim, dtype=jnp.float32) * (-2.0 * math.log(ROPE_THETA) / head_dim))
    angles = positions.astype(jnp.float32)[:, :, None] * inv_freq
    return jnp.cos(angles), jnp.sin(angles)


def rotate(values, cos_t, sin_t):
    half_dim = values.shape[-1] // 2
    lead_half = values[..., :half_dim]
    tail_half = values[..., half_dim:]
    return jnp.concatenate([lead_half * cos_t - tail_half * sin_t, tail_half * cos_t + lead_half * sin_t], axis=-1)


def norm_fwd(values):
    values_f = values.astype(jnp.float32)
    inv_rms = lax.rsqrt(jnp.mean(values_f * values_f, axis=-1, keepdims=True) + NORM_EPS)
    return values_f * inv_rms, inv_rms


def norm_bwd(grad_out, normed, inv_rms, norm_gain):
    grad_normed = grad_out * norm_gain.astype(jnp.float32)
    mean_term = jnp.mean(grad_normed * normed, axis=-1, keepdims=True)
    return inv_rms * (grad_normed - normed * mean_term)


def attn_fwd(q_rot, k_rot, v_raw):
    seq_len = q_rot.shape[1]
    attn_scale = q_rot.shape[-1] ** -0.5
    scores = jnp.einsum('bqgrh,bkgh->bgrqk', q_rot, k_rot, preferred_element_type=jnp.float32) * attn_scale
    causal = lax.broadcasted_iota(jnp.int32, (seq_len, seq_len), 0) >= lax.broadcasted_iota(jnp.int32, (seq_len, seq_len), 1)
    attn_probs = jax.nn.softmax(jnp.where(causal, scores, -1e30), axis=-1)
    attn_heads = jnp.einsum('bgrqk,bkgh->bqgrh', attn_probs.astype(jnp.bfloat16), v_raw, preferred_element_type=jnp.float32)
    return attn_heads.astype(jnp.bfloat16), attn_probs


def attn_bwd(grad_out, q_rot, k_rot, v_raw, attn_probs):
    attn_scale = q_rot.shape[-1] ** -0.5
    grad_b = grad_out.astype(jnp.bfloat16)
    probs_b = attn_probs.astype(jnp.bfloat16)
    grad_probs = jnp.einsum('bqgrh,bkgh->bgrqk', grad_b, v_raw, preferred_element_type=jnp.float32)
    grad_v = jnp.einsum('bgrqk,bqgrh->bkgh', probs_b, grad_b, preferred_element_type=jnp.float32)
    grad_scores = attn_probs * (grad_probs - jnp.sum(grad_probs * attn_probs, axis=-1, keepdims=True)) * attn_scale
    scores_b = grad_scores.astype(jnp.bfloat16)
    grad_q = jnp.einsum('bgrqk,bkgh->bqgrh', scores_b, k_rot, preferred_element_type=jnp.float32)
    grad_k = jnp.einsum('bgrqk,bqgrh->bkgh', scores_b, q_rot, preferred_element_type=jnp.float32)
    return grad_q, grad_k, grad_v


def layer_fwd(x_emb, positions, weights):
    attn_norm, w_query, w_key, w_value, q_norm, k_norm, w_out, mlp_norm, w_gate, w_up, w_down = weights
    batch_len, seq_len, model_dim = x_emb.shape
    head_dim = q_norm.shape[0]
    kv_heads = w_key.shape[1] // head_dim
    q_per_kv = w_query.shape[1] // w_key.shape[1]
    cos_t, sin_t = rope_tables(positions, head_dim)
    cos_q = cos_t[:, :, None, None, :]
    sin_q = sin_t[:, :, None, None, :]
    cos_k = cos_t[:, :, None, :]
    sin_k = sin_t[:, :, None, :]
    normed1, norm1_inv = norm_fwd(x_emb)
    attn_in = (normed1 * attn_norm.astype(jnp.float32)).astype(jnp.bfloat16)
    q_raw = jnp.einsum('bsd,dn->bsn', attn_in, w_query, preferred_element_type=jnp.float32).astype(jnp.bfloat16).reshape(batch_len, seq_len, kv_heads, q_per_kv, head_dim)
    k_raw = jnp.einsum('bsd,dn->bsn', attn_in, w_key, preferred_element_type=jnp.float32).astype(jnp.bfloat16).reshape(batch_len, seq_len, kv_heads, head_dim)
    v_raw = jnp.einsum('bsd,dn->bsn', attn_in, w_value, preferred_element_type=jnp.float32).astype(jnp.bfloat16).reshape(batch_len, seq_len, kv_heads, head_dim)
    q_normed, q_inv = norm_fwd(q_raw)
    k_normed, k_inv = norm_fwd(k_raw)
    q_rot = rotate(q_normed * q_norm.astype(jnp.float32), cos_q, sin_q).astype(jnp.bfloat16)
    k_rot = rotate(k_normed * k_norm.astype(jnp.float32), cos_k, sin_k).astype(jnp.bfloat16)
    attn_heads, attn_probs = attn_fwd(q_rot, k_rot, v_raw)
    attn_flat = attn_heads.reshape(batch_len, seq_len, -1)
    attn_proj = jnp.einsum('bsn,nd->bsd', attn_flat, w_out, preferred_element_type=jnp.float32)
    hidden = (x_emb.astype(jnp.float32) + attn_proj).astype(jnp.bfloat16)
    normed2, norm2_inv = norm_fwd(hidden)
    mlp_in = (normed2 * mlp_norm.astype(jnp.float32)).astype(jnp.bfloat16)
    gate_pre = jnp.einsum('bsd,df->bsf', mlp_in, w_gate, preferred_element_type=jnp.float32)
    up_proj = jnp.einsum('bsd,df->bsf', mlp_in, w_up, preferred_element_type=jnp.float32)
    mlp_act = (jax.nn.silu(gate_pre) * up_proj).astype(jnp.bfloat16)
    mlp_proj = jnp.einsum('bsf,fd->bsd', mlp_act, w_down, preferred_element_type=jnp.float32)
    layer_out = (hidden.astype(jnp.float32) + mlp_proj).astype(jnp.bfloat16)
    saved_acts = (normed1, norm1_inv, attn_in, q_normed, q_inv, k_normed, k_inv, q_rot, k_rot, v_raw, attn_probs, attn_flat, normed2, norm2_inv, mlp_in, gate_pre, up_proj, mlp_act, cos_q, sin_q, cos_k, sin_k)
    return layer_out, saved_acts


def layer_bwd(dy_out, saved_acts, weights):
    attn_norm, w_query, w_key, w_value, q_norm, k_norm, w_out, mlp_norm, w_gate, w_up, w_down = weights
    (normed1, norm1_inv, attn_in, q_normed, q_inv, k_normed, k_inv, q_rot, k_rot, v_raw, attn_probs, attn_flat, normed2, norm2_inv, mlp_in, gate_pre, up_proj, mlp_act, cos_q, sin_q, cos_k, sin_k) = saved_acts
    batch_len, seq_len, model_dim = dy_out.shape
    grad_w_down = jnp.einsum('bsf,bsd->fd', mlp_act, dy_out, preferred_element_type=jnp.float32)
    grad_act = jnp.einsum('bsd,fd->bsf', dy_out, w_down, preferred_element_type=jnp.float32)
    gate_sig = jax.nn.sigmoid(gate_pre)
    grad_gate = (grad_act * up_proj * gate_sig * (1.0 + gate_pre * (1.0 - gate_sig))).astype(jnp.bfloat16)
    grad_up = (grad_act * gate_pre * gate_sig).astype(jnp.bfloat16)
    grad_w_gate = jnp.einsum('bsd,bsf->df', mlp_in, grad_gate, preferred_element_type=jnp.float32)
    grad_w_up = jnp.einsum('bsd,bsf->df', mlp_in, grad_up, preferred_element_type=jnp.float32)
    grad_mlp_in = jnp.einsum('bsf,df->bsd', grad_gate, w_gate, preferred_element_type=jnp.float32) + jnp.einsum('bsf,df->bsd', grad_up, w_up, preferred_element_type=jnp.float32)
    grad_mlp_norm = jnp.sum(grad_mlp_in * normed2, axis=(0, 1))
    grad_hidden = dy_out.astype(jnp.float32) + norm_bwd(grad_mlp_in, normed2, norm2_inv, mlp_norm)
    hidden_b = grad_hidden.astype(jnp.bfloat16)
    grad_w_out = jnp.einsum('bsn,bsd->nd', attn_flat, hidden_b, preferred_element_type=jnp.float32)
    grad_heads = jnp.einsum('bsd,nd->bsn', hidden_b, w_out, preferred_element_type=jnp.float32).reshape(q_rot.shape)
    grad_q, grad_k, grad_v = attn_bwd(grad_heads, q_rot, k_rot, v_raw, attn_probs)
    grad_qt = rotate(grad_q, cos_q, -sin_q)
    grad_kt = rotate(grad_k, cos_k, -sin_k)
    grad_q_norm = jnp.sum(grad_qt * q_normed, axis=(0, 1, 2, 3))
    grad_k_norm = jnp.sum(grad_kt * k_normed, axis=(0, 1, 2))
    grad_q_raw = norm_bwd(grad_qt, q_normed, q_inv, q_norm).astype(jnp.bfloat16).reshape(batch_len, seq_len, -1)
    grad_k_raw = norm_bwd(grad_kt, k_normed, k_inv, k_norm).astype(jnp.bfloat16).reshape(batch_len, seq_len, -1)
    grad_v_raw = grad_v.astype(jnp.bfloat16).reshape(batch_len, seq_len, -1)
    grad_w_query = jnp.einsum('bsd,bsn->dn', attn_in, grad_q_raw, preferred_element_type=jnp.float32)
    grad_w_key = jnp.einsum('bsd,bsn->dn', attn_in, grad_k_raw, preferred_element_type=jnp.float32)
    grad_w_value = jnp.einsum('bsd,bsn->dn', attn_in, grad_v_raw, preferred_element_type=jnp.float32)
    grad_attn_in = (jnp.einsum('bsn,dn->bsd', grad_q_raw, w_query, preferred_element_type=jnp.float32)
                    + jnp.einsum('bsn,dn->bsd', grad_k_raw, w_key, preferred_element_type=jnp.float32)
                    + jnp.einsum('bsn,dn->bsd', grad_v_raw, w_value, preferred_element_type=jnp.float32))
    grad_attn_norm = jnp.sum(grad_attn_in * normed1, axis=(0, 1))
    grad_x_emb = grad_hidden + norm_bwd(grad_attn_in, normed1, norm1_inv, attn_norm)
    return grad_x_emb, (grad_attn_norm, grad_w_query, grad_w_key, grad_w_value, grad_q_norm, grad_k_norm, grad_w_out, grad_mlp_norm, grad_w_gate, grad_w_up, grad_w_down)


def solution(mesh):
    row_spec = P(AXIS_NAME, None)
    vec_spec = P(AXIS_NAME)
    full_spec = P(None)
    batch_spec = P(AXIS_NAME, None, None)
    weight_specs = (vec_spec, row_spec, row_spec, row_spec, full_spec, full_spec, row_spec, vec_spec, row_spec, row_spec, row_spec)

    def device_step(tokens, positions, table_shard, attn_norm, w_query, w_key, w_value, q_norm, k_norm, w_out, mlp_norm, w_gate, w_up, w_down, dy_out):
        shards = (attn_norm, w_query, w_key, w_value, q_norm, k_norm, w_out, mlp_norm, w_gate, w_up, w_down)
        weights = tuple(lax.all_gather(w_shard, AXIS_NAME, tiled=True) if is_sharded else w_shard for w_shard, is_sharded in zip(shards, SHARDED))
        batch_len, seq_len = tokens.shape
        rows_local, model_dim = table_shard.shape
        all_ids = lax.all_gather(tokens.reshape(-1), AXIS_NAME, tiled=True)
        local_ids = all_ids - lax.axis_index(AXIS_NAME) * rows_local
        is_owner = (local_ids >= 0) & (local_ids < rows_local)
        picked = jnp.take(table_shard, jnp.clip(local_ids, 0, rows_local - 1), axis=0)
        picked = jnp.where(is_owner[:, None], picked, jnp.zeros((), picked.dtype))
        x_emb = lax.psum_scatter(picked, AXIS_NAME, scatter_dimension=0, tiled=True).reshape(batch_len, seq_len, model_dim)
        layer_out, saved_acts = layer_fwd(x_emb, positions, weights)
        grad_x_emb, grad_full = layer_bwd(dy_out, saved_acts, weights)
        grad_shards = tuple(lax.psum_scatter(grad_part, AXIS_NAME, scatter_dimension=0, tiled=True) if is_sharded else lax.psum(grad_part, AXIS_NAME) for grad_part, is_sharded in zip(grad_full, SHARDED))
        all_rows = lax.all_gather(grad_x_emb.reshape(-1, model_dim), AXIS_NAME, tiled=True)
        d_table = jax.ops.segment_sum(all_rows, jnp.where(is_owner, local_ids, rows_local), num_segments=rows_local)
        return (layer_out, d_table) + grad_shards

    return jax.shard_map(device_step, mesh=mesh, in_specs=(row_spec, row_spec, row_spec) + weight_specs + (batch_spec,), out_specs=(batch_spec, row_spec) + weight_specs, check_vma=False)
```

profile of v0, /device:TPU:0, one launch (start us, length us, event | category | flops | bytes accessed | tf_op | source)
XLA Modules:
  0.0 1913.2 jit_solution(5206623819156350182)
XLA Ops:
  8.7 14.8 all_gather.33
  24.2 88.9 %gather_fusion = bf16[16384,1024]{1,0:T(8,128)(2,1)} fusion(bf16[9504,1024]{1,0:T(8,128)(2,1)} %param.17, s32[16384]{0:T(1024)S(1)} %get-tuple-element.43), kind=kCustom, calls=%fused_computation | custom fusion | bytes 67174400 | tf_op jit(solution)/shard_map/jit(_take)/gather | solution.py:148
  113.1 22.7 %select_select_fusion = bf16[16384,1024]{1,0:T(8,128)(2,1)} fusion(bf16[16384,1024]{1,0:T(8,128)(2,1)} %gather_fusion, pred[16384]{0:T(1024)(128)(4,1)S(1)} %get-tuple-element.45, pred[16384]{0:T(1024)(128)(4,1)S(1)} %get-tuple-element.44), kind=kLoop, calls=%fused_computation.11 | loop fusion | flops 33554432 | bytes 67141632 | tf_op jit(solution)/shard_map/jit(_where)/select_n | solution.py:149
  140.6 33.2 %all-reduce.5 = (bf16[1024]{0:T(1024)(128)(2,1)S(1)}, bf16[1024]{0:T(1024)(128)(2,1)S(1)}) all-reduce(bf16[1024]{0:T(1024)(128)(2,1)S(1)} %dynamic-update-slice, bf16[1024]{0:T(1024)(128)(2,1)S(1)} %dynamic-update-slice.1), channel_id=1, replica_groups=mesh['fsdp'=16] {'fsdp'}, use_global_device_ids=true, to_apply=%add | all-reduce | flops 2048 | bytes 8192
  190.0 293.5 %reduce-scatter.9.cloned.1.call-done = bf16[1024,1024]{1,0:T(8,128)(2,1)} async-done(((bf16[16384,1024]{1,0:T(8,128)(2,1)}), bf16[1024,1024]{1,0:T(8,128)(2,1)}) %reduce-scatter.9.cloned.1.call-update) | async-done | bytes 2097168 | tf_op jit(solution)/shard_map/reduce_scatter | solution.py:150
  485.6 26.7 %all-gather.9.cloned.1.call-done = bf16[1024,1024]{1,0:T(8,128)(2,1)} async-done(((bf16[64,1024]{1,0:T(8,128)(2,1)}), bf16[1024,1024]{1,0:T(8,128)(2,1)}) %all-gather.9.cloned.1.call-update) | async-done | bytes 2097168 | tf_op jit(solution)/shard_map/all_gather | solution.py:142
  518.9 23.8 %all-gather.11.cloned.1.call-done = bf16[1024,1024]{1,0:T(8,128)(2,1)} async-done(((bf16[64,1024]{1,0:T(8,128)(2,1)}), bf16[1024,1024]{1,0:T(8,128)(2,1)}) %all-gather.11.cloned.1.call-update) | async-done | bytes 2097168 | tf_op jit(solution)/shard_map/all_gather | solution.py:142
  555.0 24.9 %all-gather.13.cloned.1.call-done = bf16[1024,2048]{1,0:T(8,128)(2,1)} async-done(((bf16[64,2048]{1,0:T(8,128)(2,1)}), bf16[1024,2048]{1,0:T(8,128)(2,1)}) %all-gather.13.cloned.1.call-update) | async-done | bytes 4194320 | tf_op jit(solution)/shard_map/all_gather | solution.py:142
  631.8 20.3 %fusion.112 = (f32[2,8,2,512]{3,2,1,0:T(2,128)S(1)}, f32[2,8,2,512,512]{3,4,2,1,0:T(8,128)}) fusion(pred[512,512]{0,1:T(8,128)(4,1)S(1)} %iota_compare_fusion, bf16[2,512,8,64]{3,1,2,0:T(8,128)(2,1)} %get-tuple-element.41, bf16[2,512,8,64]{3,1,2,0:T(8,128)(2,1)S(1)} %get-tuple-element.40, bf16[2,512,8,2,64]{4,1,3,2,0:T(8,128)(2,1)} %get-tuple-element.35, ...), kind=kOutput, calls=%fused_computation.162 | convolution fusion | flops 2193621504 | bytes 40173568 | tf_op jit(solution)/shard_map/sub | solution.py:44
  652.2 15.1 fusion.65
  689.4 15.8 all-gather.17.cloned.1.call-done
  705.1 22.2 %multiply_convert_fusion.1 = (bf16[2,512,3072]{2,1,0:T(8,128)(2,1)}, bf16[2,512,3072]{2,1,0:T(8,128)(2,1)}, bf16[2,512,3072]{2,1,0:T(8,128)(2,1)}) fusion(f32[2,512,3072]{2,1,0:T(8,128)} %fusion.19, f32[2,512,3072]{2,1,0:T(8,128)} %fusion.25, bf16[1024,3072]{1,0:T(8,128)(2,1)} %all-gather.17.cloned.1.call-done, bf16[2,512,1024]{2,1,0:T(8,128)(2,1)S(1)} %copy-done.16, ...), kind=kOutput, calls=%fused_computation.23 | convolution fusion | flops 6496976896 | bytes 52436992 | tf_op jit(solution)/shard_map/bsd,df->bsf/dot_general | solution.py:88
  764.2 16.1 bitcast_convert_fusion
  780.3 15.3 fusion.95
  795.9 46.8 %fusion.75 = f32[2,512,8,128]{3,1,2,0:T(8,128)} fusion(f32[2,8,512,512,2]{3,2,4,1,0:T(8,128)} %fusion.95, bf16[2,512,8,2,64]{4,1,3,2,0:T(8,128)(2,1)} %get-tuple-element.35, bf16[2,512,8,2,64]{4,1,3,2,0:T(8,128)(2,1)} %get-tuple-element.34, f32[2,8,2,512,512]{3,4,2,1,0:T(8,128)} %get-tuple-element.50, f32[2,8,2,512]{3,2,1,0:T(2,128)S(1)} %get-tuple-element.49), kind=kOutput, calls=%fused_computation.113 | convolution fusion | flops 2214609408 | bytes 75563008 | tf_op jit(solution)/shard_map/bgrqk,bqgrh->bkgh/dot_general | solution.py:58
  842.7 46.9 %fusion.64 = f32[2,512,8,2,128]{4,1,3,2,0:T(8,128)} fusion(f32[2,8,512,512,2]{3,2,4,1,0:T(8,128)} %fusion.95, bf16[2,512,8,64]{3,1,2,0:T(8,128)(2,1)} %get-tuple-element.41, bf16[2,512,8,64]{3,1,2,0:T(8,128)(2,1)S(1)} %copy-done.20, f32[2,8,2,512,512]{3,4,2,1,0:T(8,128)} %get-tuple-element.50, f32[2,8,2,512]{3,2,1,0:T(2,128)S(1)} %get-tuple-element.49), kind=kOutput, calls=%fused_computation.110 | convolution fusion | flops 2210415104 | bytes 77660160 | tf_op jit(solution)/shard_map/bgrqk,bkgh->bqgrh/dot_general | solution.py:57
  1131.6 33.1 %all-reduce.4 = (f32[1024]{0:T(1024)S(1)}, f32[128]{0:T(128)}, f32[128]{0:T(128)}, f32[1024]{0:T(1024)S(1)}) all-reduce(f32[1024]{0:T(1024)S(1)} %get-tuple-element.15, f32[128]{0:T(128)S(1)} %reduce_sum.153, f32[128]{0:T(128)S(1)} %bitcast_reduce_fusion, f32[1024]{0:T(1024)S(1)} %copy-done.42), channel_id=3, replica_groups=mesh['fsdp'=16] {'fsdp'}, use_global_device_ids=true, to_apply=%region_14.15.clone | all-reduce | flops 2304 | bytes 18432
  1177.4 122.6 %all-gather.23.cloned.1.call-done = f32[16384,1024]{1,0:T(8,128)} async-done(((f32[1024,1024]{1,0:T(8,128)}), f32[16384,1024]{1,0:T(8,128)}) %all-gather.23.cloned.1.call-update) | async-done | bytes 67108880 | tf_op jit(solution)/shard_map/all_gather | solution.py:154
  1300.0 156.2 %scatter_custom_fusion = f32[9504,1024]{1,0:T(8,128)} fusion(s32[16384]{0:T(1024)} %get-tuple-element.42, f32[16384,1024]{1,0:T(8,128)} %all-gather.23.cloned.1.call-done, f32[]{:T(128)} %constant.22.clone.1), kind=kCustom, calls=%fused_computation.13 | custom fusion | flops 16777216 | bytes 38928896 | tf_op jit(solution)/shard_map/scatter-add | solution.py:155
  1456.2 71.5 %reduce-scatter.11.cloned.1.call-done = f32[64,2048]{1,0:T(8,128)} async-done(((f32[1024,2048]{1,0:T(8,128)}), f32[64,2048]{1,0:T(8,128)}) %reduce-scatter.11.cloned.1.call-update) | async-done | bytes 524304 | tf_op jit(solution)/shard_map/reduce_scatter | solution.py:153
  1527.7 93.8 %reduce-scatter.17.cloned.1.call-done = f32[128,1024]{1,0:T(8,128)} async-done(((f32[2048,1024]{1,0:T(8,128)}), f32[128,1024]{1,0:T(8,128)}) %reduce-scatter.17.cloned.1.call-update) | async-done | bytes 524304 | tf_op jit(solution)/shard_map/reduce_scatter | solution.py:153
  1621.5 93.7 %reduce-scatter.19.cloned.1.call-done = f32[64,3072]{1,0:T(8,128)} async-done(((f32[1024,3072]{1,0:T(8,128)}), f32[64,3072]{1,0:T(8,128)}) %reduce-scatter.19.cloned.1.call-update) | async-done | bytes 786448 | tf_op jit(solution)/shard_map/reduce_scatter | solution.py:153
  1715.2 95.5 %reduce-scatter.21.cloned.1.call-done = f32[64,3072]{1,0:T(8,128)} async-done(((f32[1024,3072]{1,0:T(8,128)}), f32[64,3072]{1,0:T(8,128)}) %reduce-scatter.21.cloned.1.call-update) | async-done | bytes 786448 | tf_op jit(solution)/shard_map/reduce_scatter | solution.py:153
  1810.7 95.5 %reduce-scatter.23.cloned.1.call-done = f32[192,1024]{1,0:T(8,128)} async-done(((f32[3072,1024]{1,0:T(8,128)}), f32[192,1024]{1,0:T(8,128)}) %reduce-scatter.23.cloned.1.call-update) | async-done | bytes 786448 | tf_op jit(solution)/shard_map/reduce_scatter | solution.py:153
  (245 shorter events, 408.8 us)
Async XLA Ops:
  7.2 170.2 %all-gather.21.cloned.1.call-start = ((), (), s32[]{:S(2)}) async-start(), calls=%async_computation.15 | async-start | bytes 6684672 | tf_op jit(solution)/shard_map/all_gather | solution.py:142
  7.9 475.6 %reduce-scatter.9.cloned.1.call-start = ((), (), s32[]{:S(2)}) async-start(), calls=%async_computation.8 | async-start | bytes 35651584 | tf_op jit(solution)/shard_map/reduce_scatter | solution.py:150
  135.9 376.4 %all-gather.9.cloned.1.call-start = ((), (), s32[]{:S(2)}) async-start(), calls=%async_computation.9 | async-start | bytes 2228224 | tf_op jit(solution)/shard_map/all_gather | solution.py:142
  136.7 406.1 %all-gather.11.cloned.1.call-start = ((), (), s32[]{:S(2)}) async-start(), calls=%async_computation.10 | async-start | bytes 2228224 | tf_op jit(solution)/shard_map/all_gather | solution.py:142
  137.2 442.7 %all-gather.13.cloned.1.call-start = ((), (), s32[]{:S(2)}) async-start(), calls=%async_computation.11 | async-start | bytes 4456448 | tf_op jit(solution)/shard_map/all_gather | solution.py:142
  137.8 529.4 %all-gather.15.cloned.1.call-start = ((), (), s32[]{:S(2)}) async-start(), calls=%async_computation.12 | async-start | bytes 4456448 | tf_op jit(solution)/shard_map/all_gather | solution.py:142
  138.4 538.5 %all-gather.19.cloned.1.call-start = ((), (), s32[]{:S(2)}) async-start(), calls=%async_computation.14 | async-start | bytes 6684672 | tf_op jit(solution)/shard_map/all_gather | solution.py:142
  139.2 566.0 %all-gather.17.cloned.1.call-start = ((), (), s32[]{:S(2)}) async-start(), calls=%async_computation.13 | async-start | bytes 6684672 | tf_op jit(solution)/shard_map/all_gather | solution.py:142
  139.9 1160.1 %all-gather.23.cloned.1.call-start = ((), (), s32[]{:S(2)}) async-start(), calls=%async_computation.16 | async-start | bytes 71303168 | tf_op jit(solution)/shard_map/all_gather | solution.py:154
  173.8 406.1 %copy-start.30 = (f32[1024]{0:T(1024)}, f32[1024]{0:T(1024)S(1)}, u32[]{:S(2)}) copy-start(f32[1024]{0:T(1024)S(1)} %convert_element_type.133) | copy-start | bytes 12292
  173.8 377.3 %copy-start.39 = (f32[128]{0:T(128)}, f32[128]{0:T(128)S(1)}, u32[]{:S(2)}) copy-start(f32[128]{0:T(128)S(1)} %convert_element_type.139) | copy-start | bytes 1540
  173.8 450.2 %copy-start.43 = (f32[128]{0:T(128)}, f32[128]{0:T(128)S(1)}, u32[]{:S(2)}) copy-start(f32[128]{0:T(128)S(1)} %convert_element_type.144) | copy-start | bytes 1540
  173.9 574.6 %copy-start.32 = (f32[1024]{0:T(1024)}, f32[1024]{0:T(1024)S(1)}, u32[]{:S(2)}) copy-start(f32[1024]{0:T(1024)S(1)} %convert_element_type.150) | copy-start | bytes 12292
  177.4 449.4 %copy-start.7 = (f32[2,512,64]{2,1,0:T(8,128)}, f32[2,512,64]{2,1,0:T(8,128)S(1)}, u32[]{:S(2)}) copy-start(f32[2,512,64]{2,1,0:T(8,128)S(1)} %get-tuple-element.48) | copy-start | bytes 786436
  485.6 94.3 %copy-start.36 = (f32[2,512]{1,0:T(2,128)}, f32[2,512]{1,0:T(2,128)S(1)}, u32[]{:S(2)}) copy-start(f32[2,512]{1,0:T(2,128)S(1)} %rsqrt.37) | copy-start | bytes 12292
  676.9 71.5 %copy-start.34 = (f32[2,512]{1,0:T(2,128)}, f32[2,512]{1,0:T(2,128)S(1)}, u32[]{:S(2)}) copy-start(f32[2,512]{1,0:T(2,128)S(1)} %add_rsqrt_fusion.2) | copy-start | bytes 12292
  842.7 46.9 %copy-start.25 = (f32[2,512,8,2]{1,2,3,0:T(8,128)S(1)}, f32[2,512,8,2]{1,2,3,0:T(8,128)}, u32[]{:S(2)}) copy-start(f32[2,512,8,2]{1,2,3,0:T(8,128)} %copy-done.24) | copy-start | bytes 196612
  1056.2 400.0 %reduce-scatter.13.cloned.1.call-start = ((), (), s32[]{:S(2)}) async-start(), calls=%async_computation.18 | async-start | bytes 4456448 | tf_op jit(solution)/shard_map/reduce_scatter | solution.py:153
  1062.5 393.7 %reduce-scatter.15.cloned.1.call-start = ((), (), s32[]{:S(2)}) async-start(), calls=%async_computation.19 | async-start | bytes 4456448 | tf_op jit(solution)/shard_map/reduce_scatter | solution.py:153
  1069.2 458.5 %reduce-scatter.11.cloned.1.call-start = ((), (), s32[]{:S(2)}) async-start(), calls=%async_computation.17 | async-start | bytes 8912896 | tf_op jit(solution)/shard_map/reduce_scatter | solution.py:153
  1078.5 543.0 %reduce-scatter.17.cloned.1.call-start = ((), (), s32[]{:S(2)}) async-start(), calls=%async_computation.20 | async-start | bytes 8912896 | tf_op jit(solution)/shard_map/reduce_scatter | solution.py:153
  1089.8 625.5 %reduce-scatter.19.cloned.1.call-start = ((), (), s32[]{:S(2)}) async-start(), calls=%async_computation.21 | async-start | bytes 13369344 | tf_op jit(solution)/shard_map/reduce_scatter | solution.py:153
  1104.1 706.7 %reduce-scatter.21.cloned.1.call-start = ((), (), s32[]{:S(2)}) async-start(), calls=%async_computation.22 | async-start | bytes 13369344 | tf_op jit(solution)/shard_map/reduce_scatter | solution.py:153
  1116.9 789.4 %reduce-scatter.23.cloned.1.call-start = ((), (), s32[]{:S(2)}) async-start(), calls=%async_computation.23 | async-start | bytes 13369344 | tf_op jit(solution)/shard_map/reduce_scatter | solution.py:153
  (51 other events, 561.0 us)
Sparse Core Ops, SparseCore 0:
  10.2 44.7 all-gather.20
  136.0 347.3 reduce-scatter.8
  485.7 26.5 all-gather.8
  514.4 28.2 all-gather.10
  544.9 35.0 all-gather.12
  582.0 35.0 all-gather.14
  619.3 41.7 all-gather.18
  663.3 41.7 all-gather.16
  1056.3 243.6 all-gather.22
  1302.7 63.8 reduce-scatter.12
  1369.5 63.2 reduce-scatter.14
  1435.5 92.1 reduce-scatter.10
  1530.5 90.9 reduce-scatter.16
  1626.6 88.6 reduce-scatter.18
  1720.3 90.4 reduce-scatter.20
  1815.8 90.4 reduce-scatter.22
where the time goes:
time: 1920 us; the launch traced here: 1910 us
  waiting for transfers between devices  962 us (50%)
  matrix products  365 us (19%)
  other arithmetic  265 us (14%)
  local copies, waits for them, and re-layouts  224 us (12%)
  blocking collectives  81.1 us (4%)
    reduce_scatter x7, waiting for transfers between devices, device_step(): lax.psum_scatter(grad_part, AXIS_NAME, scatter_dimension=0, tiled=True)  450 us
    reduce_scatter x1, waiting for transfers between devices, device_step(): lax.psum_scatter(picked, AXIS_NAME, scatter_dimension=0, tiled=True)  293 us
    scatter-add x1, other arithmetic, device_step(): jax.ops.segment_sum(all_rows, jnp.where(is_owner, local_ids, rows_local),...  156 us
    all_gather x1, waiting for transfers between devices, device_step(): lax.all_gather(grad_x_emb.reshape(-1, model_dim), AXIS_NAME, tiled=True)  123 us
    all_gather x7, waiting for transfers between devices, device_step(): lax.all_gather(w_shard, AXIS_NAME, tiled=True)  91.3 us
    gather x1, local copies, waits for them, and re-layouts, device_step(): jnp.take(table_shard, jnp.clip(local_ids, 0, rows_local - 1), axis=0)  88.9 us
    unnamed x2, blocking collectives  66.3 us
    dot_general x1, matrix products, attn_bwd(): jnp.einsum('bgrqk,bkgh->bqgrh', scores_b, k_rot, preferred_element_type=j...  46.9 us
  transfers between devices with their start and end apart: 16, of which 11 were waited for; matrix products, arithmetic and copies ran while one was open for 26% of the time, Pallas kernels for 0%

commit v1 on v0

v1 whole, which is shorter than its diff:
```python
import functools
import math
import jax
import jax.numpy as jnp
from jax import lax
from jax.experimental import pallas as pl
from jax.experimental.layout import Layout, with_layout_constraint
from jax.experimental.pallas import tpu as pltpu
from jax.sharding import PartitionSpec as P

NORM_EPS = 1e-6
ROPE_THETA = 1.0e6
AXIS_NAME = 'fsdp'
NEG = -1e30


def split_rows(a):
    return a.reshape(2, a.shape[0] // 2, a.shape[1])


def kdot_nn(a, b):
    return lax.dot_general(a, b, (((1,), (0,)), ((), ())), preferred_element_type=jnp.float32)


def kdot_nt(a, b):
    return lax.dot_general(a, b, (((1,), (1,)), ((), ())), preferred_element_type=jnp.float32)


def dot_nn(a, b):
    return lax.dot_general(split_rows(a), b, (((2,), (0,)), ((), ())), preferred_element_type=jnp.float32).reshape(a.shape[0], -1)


def dot_nt(a, b):
    return lax.dot_general(split_rows(a), b, (((2,), (1,)), ((), ())), preferred_element_type=jnp.float32).reshape(a.shape[0], -1)


def dot_tn(a, b):
    return lax.dot_general(split_rows(a), split_rows(b), (((0, 1), (0, 1)), ((), ())), preferred_element_type=jnp.float32)


def row_major(a):
    return with_layout_constraint(a, Layout(major_to_minor=tuple(range(a.ndim))))


def norm_fwd(values):
    values_f = values.astype(jnp.float32)
    inv_rms = lax.rsqrt(jnp.mean(values_f * values_f, axis=-1, keepdims=True) + NORM_EPS)
    return values_f * inv_rms, inv_rms


def norm_bwd(grad_out, normed, inv_rms, gain_f):
    grad_normed = grad_out * gain_f
    mean_term = jnp.mean(grad_normed * normed, axis=-1, keepdims=True)
    return inv_rms * (grad_normed - normed * mean_term)


def rope_tables(positions, head_dim):
    half_dim = head_dim // 2
    inv_freq = jnp.exp(jnp.arange(half_dim, dtype=jnp.float32) * (-2.0 * math.log(ROPE_THETA) / head_dim))
    angles = positions.astype(jnp.float32).reshape(-1, 1) * inv_freq
    cos_t, sin_t = jnp.cos(angles), jnp.sin(angles)
    return jnp.concatenate([cos_t, cos_t], axis=-1), jnp.concatenate([-sin_t, sin_t], axis=-1)


def rope(values, cos_t, sin_t):
    return values * cos_t + pltpu.roll(values, values.shape[-1] // 2, 1) * sin_t


def attn_fwd_kernel(n_rep, hd, chunk, qkv_ref, cos_ref, sin_ref, qg_ref, kg_ref, out_ref, *rep_refs):
    seq = qkv_ref.shape[0]
    scale = hd ** -0.5
    cos_t, sin_t = cos_ref[...], sin_ref[...]
    k_n, _ = norm_fwd(qkv_ref[:, n_rep * hd:(n_rep + 1) * hd])
    k_rot = rope(k_n * kg_ref[...], cos_t, sin_t).astype(jnp.bfloat16)
    v_raw = qkv_ref[:, (n_rep + 1) * hd:(n_rep + 2) * hd]
    for rep in range(n_rep):
        q_n, _ = norm_fwd(qkv_ref[:, rep * hd:(rep + 1) * hd])
        q_rot = rope(q_n * qg_ref[...], cos_t, sin_t).astype(jnp.bfloat16)
        for lo in range(0, seq, chunk):
            end = lo + chunk
            s = kdot_nt(q_rot[lo:end], k_rot[:end]) * scale
            rows = lax.broadcasted_iota(jnp.int32, s.shape, 0) + lo
            cols = lax.broadcasted_iota(jnp.int32, s.shape, 1)
            s = jnp.where(rows >= cols, s, NEG)
            e = jnp.exp(s - jnp.max(s, axis=-1, keepdims=True))
            p = e * (1.0 / jnp.sum(e, axis=-1, keepdims=True))
            o = kdot_nn(p.astype(jnp.bfloat16), v_raw[:end])
            out_ref[lo:end, rep * hd:(rep + 1) * hd] = o.astype(jnp.bfloat16)
            rep_refs[rep][lo:end] = o.astype(jnp.bfloat16)


def attn_fwd(qkv, cos_t, sin_t, q_gain, k_gain, batch, kv_heads, n_rep, hd):
    tokens, width = qkv.shape
    seq = tokens // batch
    gw = width // kv_heads
    return pl.pallas_call(
        functools.partial(attn_fwd_kernel, n_rep, hd, seq // 2),
        grid=(batch, kv_heads),
        in_specs=[pl.BlockSpec((seq, gw), lambda b, g: (b, g)),
                  pl.BlockSpec((seq, hd), lambda b, g: (b, 0)),
                  pl.BlockSpec((seq, hd), lambda b, g: (b, 0)),
                  pl.BlockSpec((1, hd), lambda b, g: (0, 0)),
                  pl.BlockSpec((1, hd), lambda b, g: (0, 0))],
        out_specs=[pl.BlockSpec((seq, n_rep * hd), lambda b, g: (b, g))] + [pl.BlockSpec((seq, hd), lambda b, g: (b, g))] * n_rep,
        out_shape=[jax.ShapeDtypeStruct((tokens, kv_heads * n_rep * hd), jnp.bfloat16)] + [jax.ShapeDtypeStruct((tokens, kv_heads * hd), jnp.bfloat16)] * n_rep,
        cost_estimate=pl.CostEstimate(flops=25_000_000_000, bytes_accessed=14_000_000, transcendentals=8_400_000),
        name='attn_fwd',
    )(qkv, cos_t, sin_t, q_gain, k_gain)


def attn_bwd_kernel(n_rep, hd, chunk, n_alias, qkv_ref, do_ref, cos_ref, sin_ref, qg_ref, kg_ref, *rest):
    dqkv_ref, dqg_ref, dkg_ref, dk_acc, dv_acc = rest[n_alias:]
    seq = qkv_ref.shape[0]
    scale = hd ** -0.5
    cos_t, sin_t = cos_ref[...], sin_ref[...]
    qg, kg = qg_ref[...], kg_ref[...]

    @pl.when(pl.program_id(0) == 0)
    def _():
        dqg_ref[...] = jnp.zeros_like(dqg_ref)
        dkg_ref[...] = jnp.zeros_like(dkg_ref)

    k_n, k_inv = norm_fwd(qkv_ref[:, n_rep * hd:(n_rep + 1) * hd])
    k_rot_f = rope(k_n * kg, cos_t, sin_t)
    k_rot = k_rot_f.astype(jnp.bfloat16)
    k_rot_t = k_rot_f.T.astype(jnp.bfloat16)
    v_raw = qkv_ref[:, (n_rep + 1) * hd:(n_rep + 2) * hd]
    dk_acc[...] = jnp.zeros_like(dk_acc)
    dv_acc[...] = jnp.zeros_like(dv_acc)
    for rep in range(n_rep):
        q_n, q_inv = norm_fwd(qkv_ref[:, rep * hd:(rep + 1) * hd])
        q_rot = rope(q_n * qg, cos_t, sin_t).astype(jnp.bfloat16)
        dq_parts = []
        for lo in range(0, seq, chunk):
            end = lo + chunk
            q_c = q_rot[lo:end]
            do_c = do_ref[lo:end, rep * hd:(rep + 1) * hd]
            s = kdot_nt(k_rot[:end], q_c) * scale
            keys = lax.broadcasted_iota(jnp.int32, s.shape, 0)
            qpos = lax.broadcasted_iota(jnp.int32, s.shape, 1) + lo
            s = jnp.where(qpos >= keys, s, NEG)
            e = jnp.exp(s - jnp.max(s, axis=0, keepdims=True))
            p = e * (1.0 / jnp.sum(e, axis=0, keepdims=True))
            dv_acc[:end] += kdot_nn(p.astype(jnp.bfloat16), do_c)
            dp = kdot_nt(v_raw[:end], do_c)
            delta = jnp.sum(dp * p, axis=0, keepdims=True)
            ds = (p * (dp - delta) * scale).astype(jnp.bfloat16)
            dk_acc[:end] += kdot_nn(ds, q_c)
            dq_parts.append(kdot_nn(k_rot_t[:, :end], ds).T)
        dq = jnp.concatenate(dq_parts, axis=0)
        dqt = dq * cos_t - pltpu.roll(dq, hd // 2, 1) * sin_t
        dqg_ref[...] += jnp.sum((dqt * q_n).reshape(seq // 8, 8, hd), axis=0)
        dqkv_ref[:, rep * hd:(rep + 1) * hd] = norm_bwd(dqt, q_n, q_inv, qg).astype(jnp.bfloat16)
    dk = dk_acc[...]
    dkt = dk * cos_t - pltpu.roll(dk, hd // 2, 1) * sin_t
    dkg_ref[...] += jnp.sum((dkt * k_n).reshape(seq // 8, 8, hd), axis=0)
    dqkv_ref[:, n_rep * hd:(n_rep + 1) * hd] = norm_bwd(dkt, k_n, k_inv, kg).astype(jnp.bfloat16)
    dqkv_ref[:, (n_rep + 1) * hd:(n_rep + 2) * hd] = dv_acc[...].astype(jnp.bfloat16)


def attn_bwd(b, prev, qkv, do, cos_t, sin_t, q_gain, k_gain, batch, kv_heads, n_rep, hd):
    tokens, width = qkv.shape
    seq = tokens // batch
    gw = width // kv_heads
    return pl.pallas_call(
        functools.partial(attn_bwd_kernel, n_rep, hd, seq // 2, len(prev)),
        grid=(kv_heads,),
        in_specs=[pl.BlockSpec((seq, gw), lambda g: (b, g)),
                  pl.BlockSpec((seq, n_rep * hd), lambda g: (b, g)),
                  pl.BlockSpec((seq, hd), lambda g: (b, 0)),
                  pl.BlockSpec((seq, hd), lambda g: (b, 0)),
                  pl.BlockSpec((1, hd), lambda g: (0, 0)),
                  pl.BlockSpec((1, hd), lambda g: (0, 0))] + [pl.BlockSpec(memory_space=pl.ANY)] * len(prev),
        out_specs=[pl.BlockSpec((seq, gw), lambda g: (b, g)),
                   pl.BlockSpec((8, hd), lambda g: (0, 0)),
                   pl.BlockSpec((8, hd), lambda g: (0, 0))],
        out_shape=[jax.ShapeDtypeStruct((tokens, width), jnp.bfloat16),
                   jax.ShapeDtypeStruct((8, hd), jnp.float32),
                   jax.ShapeDtypeStruct((8, hd), jnp.float32)],
        input_output_aliases={6: 0} if prev else {},
        scratch_shapes=[pltpu.VMEM((seq, hd), jnp.float32), pltpu.VMEM((seq, hd), jnp.float32)],
        cost_estimate=pl.CostEstimate(flops=25_000_000_000, bytes_accessed=14_000_000, transcendentals=4_200_000),
        name='attn_bwd',
    )(qkv, do, cos_t, sin_t, q_gain, k_gain, *prev)


def mlp_bwd_kernel(ff, gu_ref, ga_ref, out_ref, act_ref, act_t_ref):
    gate, up, grad_act = gu_ref[:, :ff], gu_ref[:, ff:], ga_ref[...]
    sig = jax.nn.sigmoid(gate)
    out_ref[:, :ff] = (grad_act * up * sig * (1.0 + gate * (1.0 - sig))).astype(jnp.bfloat16)
    out_ref[:, ff:] = (grad_act * gate * sig).astype(jnp.bfloat16)
    act = gate * sig * up
    act_ref[...] = act.astype(jnp.bfloat16)
    act_t_ref[...] = act.T.astype(jnp.bfloat16)


def mlp_bwd(gu, grad_act):
    tokens, ff = grad_act.shape
    rows = 128
    return pl.pallas_call(
        functools.partial(mlp_bwd_kernel, ff),
        grid=(tokens // rows,),
        in_specs=[pl.BlockSpec((rows, 2 * ff), lambda i: (i, 0)), pl.BlockSpec((rows, ff), lambda i: (i, 0))],
        out_specs=[pl.BlockSpec((rows, 2 * ff), lambda i: (i, 0)), pl.BlockSpec((rows, ff), lambda i: (i, 0)), pl.BlockSpec((ff, rows), lambda i: (0, i))],
        out_shape=[jax.ShapeDtypeStruct((tokens, 2 * ff), jnp.bfloat16), jax.ShapeDtypeStruct((tokens, ff), jnp.bfloat16), jax.ShapeDtypeStruct((ff, tokens), jnp.bfloat16)],
        cost_estimate=pl.CostEstimate(flops=16_000_000_000, bytes_accessed=50_000_000, transcendentals=3_200_000),
        name='mlp_bwd',
    )(gu, grad_act)


def solution(mesh):
    n_dev = mesh.shape[AXIS_NAME]
    n_chip = n_dev // 2
    pairs = [(i, i ^ 1) for i in range(n_dev)]
    same_core = [[2 * k + core for k in range(n_chip)] for core in range(2)]
    row_spec = P(AXIS_NAME, None)
    vec_spec = P(AXIS_NAME)
    full_spec = P(None)
    batch_spec = P(AXIS_NAME, None, None)
    weight_specs = (vec_spec, row_spec, row_spec, row_spec, full_spec, full_spec, row_spec, vec_spec, row_spec, row_spec, row_spec)

    def gather(shard):
        return lax.all_gather(shard, AXIS_NAME, tiled=True)

    def scatter_chips(part):
        return lax.psum_scatter(part, AXIS_NAME, scatter_dimension=0, tiled=True, axis_index_groups=same_core)

    def swap_core(part):
        return lax.ppermute(part, AXIS_NAME, pairs)

    def device_step(tokens, positions, table_shard, attn_norm, w_query, w_key, w_value, q_norm, k_norm, w_out, mlp_norm, w_gate, w_up, w_down, dy_out):
        me = lax.axis_index(AXIS_NAME)
        core = lax.rem(me, 2)
        batch, seq = tokens.shape
        rows_local, dim = table_shard.shape
        n_tok = batch * seq
        hd = q_norm.shape[0]
        kv_heads = w_key.shape[1] // hd
        n_rep = w_query.shape[1] // w_key.shape[1]
        ff = w_gate.shape[1]
        shard_rows = w_query.shape[0]

        def near_far(blocks, axis):
            return lax.dynamic_index_in_dim(blocks, core, axis, False), lax.dynamic_index_in_dim(blocks, 1 - core, axis, False)

        small = jnp.concatenate([tokens.reshape(-1).astype(jnp.float32), attn_norm.astype(jnp.float32), mlp_norm.astype(jnp.float32)])
        small = lax.all_gather(small, AXIS_NAME)
        attn_gain = small[:, n_tok:n_tok + shard_rows].reshape(1, dim)
        mlp_gain = small[:, n_tok + shard_rows:].reshape(1, dim)

        def group_columns(w):
            return w.reshape(w.shape[0], kv_heads, -1)

        qkv_shard = jnp.concatenate([group_columns(w_query), group_columns(w_key), group_columns(w_value)], axis=2).reshape(shard_rows, -1)
        gu_shard = jnp.concatenate([w_gate, w_up], axis=1)
        wqkv = gather(qkv_shard)
        small, gu_shard, _ = lax.optimization_barrier((small, gu_shard, qkv_shard))
        all_ids = small[:, :n_tok].astype(jnp.int32).reshape(n_chip, 2, batch, seq)

        def local_rows(ids, owner):
            local = ids - owner * rows_local
            return local, ((local >= 0) & (local < rows_local))[:, None]

        def pick(ids):
            local, _ = local_rows(ids, me)
            return jnp.take(table_shard, jnp.clip(local, 0, rows_local - 1), axis=0, mode='clip')

        seq_pad = -(-seq // 48) * 48

        def lookup(b):
            ids = jnp.pad(all_ids[:, :, b], ((0, 0), (0, 0), (0, seq_pad - seq)), constant_values=-1)
            near, far = near_far(ids, 1)
            near, far = near.reshape(-1), far.reshape(-1)
            recv = swap_core(pick(far))
            zero = jnp.zeros((), table_shard.dtype)
            merged = jnp.where(local_rows(near, me)[1], pick(near), jnp.where(local_rows(near, me + 1 - 2 * core)[1], recv, zero))
            return merged

        wo = gather(w_out)
        merged = []
        for b in range(batch):
            merged.append(lookup(b))
            merged[b], all_ids = lax.optimization_barrier((merged[b], all_ids))
        merged[-1], gu_shard, w_down = lax.optimization_barrier((merged[-1], gu_shard, w_down))
        x_emb = jnp.concatenate([scatter_chips(m)[:seq] for m in merged], axis=0)
        wgu = gather(gu_shard)
        wdown = gather(w_down)

        cos_t, sin_t = rope_tables(positions, hd)
        q_gain = q_norm.astype(jnp.float32)[None]
        k_gain = k_norm.astype(jnp.float32)[None]

        normed1, norm1_inv = norm_fwd(x_emb)
        attn_in = (normed1 * attn_gain).astype(jnp.bfloat16)
        qkv = dot_nn(attn_in, wqkv).astype(jnp.bfloat16)
        heads, *heads_rep = attn_fwd(qkv, cos_t, sin_t, q_gain, k_gain, batch, kv_heads, n_rep, hd)
        hidden = (x_emb.astype(jnp.float32) + dot_nn(heads, wo)).astype(jnp.bfloat16)
        normed2, norm2_inv = norm_fwd(hidden)
        mlp_in = (normed2 * mlp_gain).astype(jnp.bfloat16)
        gu = dot_nn(mlp_in, wgu)

        dy = dy_out.reshape(n_tok, dim)
        grad_act = dot_nt(dy, wdown)
        dgu, act, act_t = mlp_bwd(gu, grad_act)

        row_ids = jnp.arange(dim)

        def split_cores(a, block):
            pad = jnp.full((n_chip, 2, block - shard_rows), -1, row_ids.dtype)
            order = jnp.concatenate([row_ids.reshape(n_chip, 2, shard_rows), pad], axis=2)
            order = jnp.concatenate([part.reshape(-1) for part in near_far(order, 1)])
            select = (row_ids[:, None] == order[None, :]).astype(jnp.bfloat16)
            both = dot_nn(a, select).astype(jnp.bfloat16)
            return both[:, :n_chip * block], both[:, n_chip * block:]

        near2, far2 = split_cores(mlp_in, shard_rows)
        near_down, far_down = near_far(kdot_nn(act_t, dy).reshape(n_chip, 2, -1, dim), 1)
        part_down = near_down.reshape(-1, dim) + swap_core(far_down.reshape(-1, dim))
        far_gu, part_down, dgu = lax.optimization_barrier((dot_tn(far2, dgu), part_down, dgu))
        g_down = scatter_chips(part_down)
        recv_gu = swap_core(far_gu)
        grad_mlp_in = dot_nt(dgu, wgu)
        part_gu = dot_tn(near2, dgu) + recv_gu
        grad_mlp_norm = jnp.sum(grad_mlp_in * normed2, axis=0)
        grad_hidden = dy.astype(jnp.float32) + norm_bwd(grad_mlp_in, normed2, norm2_inv, mlp_gain)
        hidden_b = grad_hidden.astype(jnp.bfloat16)
        hidden_b, part_gu = lax.optimization_barrier((hidden_b, part_gu))
        g_gu = scatter_chips(part_gu)

        hidden_pad = jnp.pad(hidden_b, ((0, 0), (0, -dim % 384)))
        near_h = jnp.where(core == 0, heads_rep[0], heads_rep[1])
        far_h = jnp.where(core == 0, heads_rep[1], heads_rep[0])
        recv_out = swap_core(dot_tn(far_h, hidden_pad))
        grad_heads = dot_nt(hidden_b, wo).astype(jnp.bfloat16)
        part_out = dot_tn(near_h, hidden_pad) + recv_out
        grad_heads, part_out = lax.optimization_barrier((grad_heads, part_out))
        g_out = scatter_chips(part_out)[:, :dim]
        local_ids = (all_ids - me * rows_local).reshape(n_dev, batch, seq)
        slots = jnp.where((local_ids >= 0) & (local_ids < rows_local), local_ids, rows_local)
        grad_attn_norm, grad_q_norm, grad_k_norm = 0.0, 0.0, 0.0
        dqkv, all_rows = (), []
        for b in range(batch):
            rows = slice(b * seq, (b + 1) * seq)
            dqkv, dqg, dkg = attn_bwd(b, dqkv, qkv, grad_heads, cos_t, sin_t, q_gain, k_gain, batch, kv_heads, n_rep, hd)
            grad_attn_in = dot_nt(dqkv[rows], wqkv)
            grad_attn_norm += jnp.sum(grad_attn_in * normed1[rows], axis=0)
            grad_q_norm += jnp.sum(dqg, axis=0)
            grad_k_norm += jnp.sum(dkg, axis=0)
            grad_x = grad_hidden[rows] + norm_bwd(grad_attn_in, normed1[rows], norm1_inv[rows], attn_gain)
            grad_x, dqkv = lax.optimization_barrier((row_major(grad_x), dqkv))
            all_rows.append(gather(grad_x))
            dqkv = (dqkv,)
        dqkv, = dqkv
        near1, far1 = split_cores(attn_in, -(-shard_rows // 24) * 24)
        part_qkv = dot_tn(near1, dqkv) + swap_core(dot_tn(far1, dqkv))
        g_qkv = scatter_chips(part_qkv)[:shard_rows]
        layer_out = (hidden.astype(jnp.float32) + dot_nn(act, wdown)).astype(jnp.bfloat16)

        vec = jnp.concatenate([grad_attn_norm, grad_mlp_norm, grad_q_norm, grad_k_norm])
        vec, part_qkv, layer_out = lax.optimization_barrier((vec, part_qkv, layer_out))
        vec = jnp.sum(lax.all_gather(vec, AXIS_NAME), axis=0)
        g_attn_norm = lax.dynamic_slice_in_dim(vec[:dim], me * shard_rows, shard_rows)
        g_mlp_norm = lax.dynamic_slice_in_dim(vec[dim:2 * dim], me * shard_rows, shard_rows)
        g_q_norm = vec[2 * dim:2 * dim + hd]
        g_k_norm = vec[2 * dim + hd:]

        d_table = jnp.zeros((rows_local, dim), jnp.float32)
        for b in range(batch):
            d_table = d_table.at[slots[:, b].reshape(-1)].add(all_rows[b], mode='drop')

        g_qkv = g_qkv.reshape(shard_rows, kv_heads, n_rep + 2, hd)
        g_query = g_qkv[:, :, :n_rep].reshape(shard_rows, -1)
        g_key = g_qkv[:, :, n_rep].reshape(shard_rows, -1)
        g_value = g_qkv[:, :, n_rep + 1].reshape(shard_rows, -1)
        return (layer_out.reshape(dy_out.shape), d_table, g_attn_norm, g_query, g_key, g_value, g_q_norm, g_k_norm, g_out, g_mlp_norm, g_gu[:, :ff], g_gu[:, ff:], g_down)

    return jax.shard_map(device_step, mesh=mesh, in_specs=(row_spec, row_spec, row_spec) + weight_specs + (batch_spec,), out_specs=(batch_spec, row_spec) + weight_specs, check_vma=False)
```

time: 1920 us -> 1130 us (0.59)
  waiting for transfers between devices: 962 us -> 348 us
  matrix products: 365 us -> 203 us
  Pallas kernels: 0 us -> 139 us
  local copies, waits for them, and re-layouts: 224 us -> 151 us
  blocking collectives: 81.1 us -> 28.7 us
  other arithmetic: 265 us -> 231 us
    reduce_scatter x8 -> x6, waiting for transfers between devices: 744 us -> 275 us  [scatter_chips(): lax.psum_scatter(part, AXIS_NAME, scatter_dimension=0, tiled=True, axis_i...]
    all_gather x8 -> x6, waiting for transfers between devices: 214 us -> 52.5 us  [gather(): return lax.all_gather(shard, AXIS_NAME, tiled=True)]
    dot_general x26 -> x18, matrix products: 345 us -> 203 us  [the longest x6 68.4 us: dot_nn(): lax.dot_general(split_rows(a), b, (((2,), (0,)), ((), ())), preferred_ele...]
    pallas_call x0 -> x4, Pallas kernels: none -> 139 us  [the longest x2 67.3 us: attn_bwd(): pl.pallas_call(functools.partial(attn_bwd_kernel, n_rep, hd, seq // 2, le...]
    unnamed x2 -> x0, blocking collectives: 66.3 us -> none
    mul x10 -> x2, local copies, waits for them, and re-layouts: 64.8 us -> 0.14 us  [the longest x1 0.07 us: device_step(): mlp_in = (normed2 * mlp_gain).astype(jnp.bfloat16)]
    scatter-add x1 -> x2, other arithmetic: 156 us -> 185 us  [device_step(): d_table = d_table.at[slots[:, b].reshape(-1)].add(all_rows[b], mode='drop')]
    reduce_sum x5, other arithmetic: 28.6 us -> 0.17 us  [the longest x1 0.1 us: device_step(): vec = jnp.sum(lax.all_gather(vec, AXIS_NAME), axis=0)]
  transfers between devices with their start and end apart: 16 -> 18, of which waited for: 11 -> 6; matrix products, arithmetic and copies ran while one was open for 26% -> 41% of each run, Pallas kernels for 0% -> 10%
where the time goes in v1:
time: 1130 us; the launch traced here: 1120 us
  waiting for transfers between devices  348 us (31%)
  other arithmetic  231 us (20%)
  matrix products  203 us (18%)
  local copies, waits for them, and re-layouts  151 us (13%)
  Pallas kernels  139 us (12%)
  blocking collectives  28.7 us (3%)
  between operations  16.8 us (1%)
    reduce_scatter x6, waiting for transfers between devices, scatter_chips(): lax.psum_scatter(part, AXIS_NAME, scatter_dimension=0, tiled=True, axis_i...  275 us
    scatter-add x2, other arithmetic, device_step(): d_table = d_table.at[slots[:, b].reshape(-1)].add(all_rows[b], mode='drop')  185 us
    gather x4, local copies, waits for them, and re-layouts, pick(): jnp.take(table_shard, jnp.clip(local, 0, rows_local - 1), axis=0, mode='c...  116 us
    dot_general x6, matrix products, dot_nn(): lax.dot_general(split_rows(a), b, (((2,), (0,)), ((), ())), preferred_ele...  68.4 us
    pallas_call x2, Pallas kernels, attn_bwd(): pl.pallas_call(functools.partial(attn_bwd_kernel, n_rep, hd, seq // 2, le...  67.3 us
    dot_general x5, matrix products, dot_nt(): lax.dot_general(split_rows(a), b, (((2,), (1,)), ((), ())), preferred_ele...  62.7 us
    dot_general x6, matrix products, dot_tn(): lax.dot_general(split_rows(a), split_rows(b), (((0, 1), (0, 1)), ((), ())...  59.1 us
    all_gather x6, waiting for transfers between devices, gather(): return lax.all_gather(shard, AXIS_NAME, tiled=True)  52.5 us
  transfers between devices with their start and end apart: 18, of which 6 were waited for; matrix products, arithmetic and copies ran while one was open for 41% of the time, Pallas kernels for 10%

profile of v1, /device:TPU:0, one launch (start us, length us, event | category | flops | bytes accessed | tf_op | source)
XLA Modules:
  0.0 1119.0 jit_solution(18303084097314864726)
XLA Ops:
  10.2 14.8 %all-gather.2 = f32[16,1,1152]{2,1,0:T(1,128)S(1)} all-gather(f32[1,1,1152]{2,1,0:T(1,128)S(1)} %reshape.513), channel_id=2, replica_groups=mesh['fsdp'=16] {'fsdp'}, dimensions={0}, use_global_device_ids=true | all-gather | bytes 78336 | tf_op jit(solution)/shard_map/all_gather | solution.py:247
  31.2 28.6 %gather_fusion.1 = bf16[4224,1024]{1,0:T(8,128)(2,1)} fusion(bf16[9504,1024]{1,0:T(8,128)(2,1)} %param.17, s32[5120]{0:T(1024)S(1)} %pad_clamp_fusion.2), kind=kCustom, calls=%fused_computation.1 | custom fusion | bytes 17318400 | tf_op jit(solution)/shard_map/jit(_take)/gather | solution.py:266
  60.4 28.6 %gather_fusion = bf16[4224,1024]{1,0:T(8,128)(2,1)} fusion(bf16[9504,1024]{1,0:T(8,128)(2,1)} %param.17, s32[5120]{0:T(1024)S(1)} %pad_clamp_fusion.3), kind=kCustom, calls=%fused_computation | custom fusion | bytes 17318400 | tf_op jit(solution)/shard_map/jit(_take)/gather | solution.py:266
  99.6 29.3 %gather_fusion.3 = bf16[4224,1024]{1,0:T(8,128)(2,1)} fusion(bf16[9504,1024]{1,0:T(8,128)(2,1)} %param.17, s32[5120]{0:T(1024)S(1)} %pad_clamp_fusion), kind=kCustom, calls=%fused_computation.3 | custom fusion | bytes 17318400 | tf_op jit(solution)/shard_map/jit(_take)/gather | solution.py:266
  129.4 29.1 %gather_fusion.2 = bf16[4224,1024]{1,0:T(8,128)(2,1)} fusion(bf16[9504,1024]{1,0:T(8,128)(2,1)} %param.17, s32[5120]{0:T(1024)S(1)} %pad_clamp_fusion.1), kind=kCustom, calls=%fused_computation.2 | custom fusion | bytes 17318400 | tf_op jit(solution)/shard_map/jit(_take)/gather | solution.py:266
  177.7 37.5 %all-gather.17.cloned.1.call-done = bf16[3072,1024]{1,0:T(8,128)(2,1)} async-done(((bf16[192,1024]{1,0:T(8,128)(2,1)}), bf16[3072,1024]{1,0:T(8,128)(2,1)}) %all-gather.17.cloned.1.call-update) | async-done | bytes 6291472 | tf_op jit(solution)/shard_map/all_gather | solution.py:223
  215.2 12.9 %fusion.2 = f32[3072,2,512]{0,2,1:T(8,128)} fusion(bf16[2,512,1024]{2,1,0:T(8,128)(2,1)S(1)} %copy-done.8, bf16[3072,1024]{1,0:T(8,128)(2,1)} %all-gather.17.cloned.1.call-done), kind=kOutput, calls=%fused_computation.13 | convolution fusion | flops 6442450944 | bytes 20971520 | tf_op jit(solution)/shard_map/dot_general | solution.py:34
  228.1 68.8 %reduce-scatter.9.cloned.1.call-done = bf16[528,1024]{1,0:T(8,128)(2,1)} async-done(((bf16[4224,1024]{1,0:T(8,128)(2,1)}), bf16[528,1024]{1,0:T(8,128)(2,1)}) %reduce-scatter.9.cloned.1.call-update) | async-done | bytes 1081360 | tf_op jit(solution)/shard_map/reduce_scatter | solution.py:226
  298.8 15.6 %convolution_convert_fusion.qkv_ref = bf16[1024,4096]{1,0:T(8,128)(2,1)} fusion(bf16[1024,4096]{1,0:T(8,128)(2,1)} %all-gather.11.cloned.1.call-done, f32[1024]{0:T(1024)S(1)} %mul.184, f32[1024]{0:T(1024)S(1)} %add_rsqrt_fusion.1, bf16[512,1024]{1,0:T(8,128)(2,1)S(1)} %slice.143, bf16[512,1024]{1,0:T(8,128)(2,1)S(1)} %slice.141), kind=kOutput, calls=%fused_computation.11 | convolution fusion | flops 8601468928 | bytes 18882560 | tf_op jit(solution)/shard_map/dot_general | solution.py:30
  314.3 48.5 %attn_fwd.1 = (bf16[1024,2048]{1,0:T(8,128)(2,1)}, bf16[1024,1024]{1,0:T(8,128)(2,1)}, bf16[1024,1024]{1,0:T(8,128)(2,1)}) custom-call(bf16[1024,4096]{1,0:T(8,128)(2,1)} %convolution_convert_fusion.qkv_ref, f32[1024,128]{1,0:T(8,128)} %get-tuple-element.125.cos_ref, f32[1024,128]{1,0:T(8,128)} %get-tuple-element.126.sin_ref, ...), custom_call_target="tpu_custom_call" | custom-call | flops 24999999488 | bytes 14000000 | tf_op jit(solution)/shard_map/attn_fwd/pallas_call | solution.py:96
  372.2 14.9 %all-gather.15.cloned.1.call-done = bf16[1024,6144]{1,0:T(8,128)(2,1)} async-done(((bf16[64,6144]{1,0:T(8,128)(2,1)}), bf16[1024,6144]{1,0:T(8,128)(2,1)}) %all-gather.15.cloned.1.call-update) | async-done | bytes 12582928 | tf_op jit(solution)/shard_map/all_gather | solution.py:223
  387.0 22.0 %fusion.41.gu_ref = f32[1024,6144]{1,0:T(8,128)} fusion(bf16[1024,6144]{1,0:T(8,128)(2,1)} %all-gather.15.cloned.1.call-done, bf16[1024,1024]{1,0:T(8,128)(2,1)} %get-tuple-element.121, f32[1024]{0:T(1024)S(1)} %mul.196, f32[1024]{0:T(1024)S(1)} %add_rsqrt_fusion), kind=kOutput, calls=%fused_computation.74 | convolution fusion | flops 12889096192 | bytes 39854080 | tf_op jit(solution)/shard_map/dot_general | solution.py:30
  409.0 22.9 %mlp_bwd.1 = (bf16[1024,6144]{1,0:T(8,128)(2,1)}, bf16[1024,3072]{1,0:T(8,128)(2,1)}, bf16[3072,1024]{1,0:T(8,128)(2,1)}) custom-call(f32[1024,6144]{1,0:T(8,128)} %fusion.41.gu_ref, f32[1024,3072]{1,0:T(8,128)} %bitcast.120), custom_call_target="tpu_custom_call" | custom-call | flops 16000000000 | bytes 50000000 | tf_op jit(solution)/shard_map/mlp_bwd/pallas_call | solution.py:200
  431.9 12.6 %fusion.61 = f32[8,2,192,1024]{3,2,1,0:T(8,128)} fusion(bf16[8,2,192,1024]{3,2,1,0:T(8,128)(2,1)} %bitcast.121, bf16[1024,1024,1,1]{1,0,3,2:T(8,128)(2,1)S(1)} %bitcast.99), kind=kOutput, calls=%fused_computation.140 | convolution fusion | flops 6442450944 | bytes 20971520 | tf_op jit(solution)/shard_map/dot_general | solution.py:22
  460.9 14.5 %fusion.39 = f32[512,6144]{1,0:T(8,128)} fusion(bf16[1024,6144]{1,0:T(8,128)(2,1)} %get-tuple-element.58, bf16[1024,1024]{1,0:T(8,128)(2,1)S(1)} %fusion.34), kind=kOutput, calls=%fused_computation.69 | convolution fusion | flops 6442450944 | bytes 26214400 | tf_op jit(solution)/shard_map/dot_general | solution.py:38
  482.6 22.6 %fusion.16 = (f32[1024]{0:T(1024)}, f32[1024]{0:T(1024)S(1)}, f32[1024,1024]{1,0:T(8,128)S(1)}) fusion(bf16[1024,1024]{1,0:T(8,128)(2,1)} %get-tuple-element.121, f32[1024]{0:T(1024)S(1)} %add_rsqrt_fusion, f32[1024]{0:T(1024)S(1)} %mul.196, bf16[1024,6144]{1,0:T(8,128)(2,1)} %get-tuple-element.58, bf16[1024,6144]{1,0:T(8,128)(2,1)} %all-gather.15.cloned.1.call-done), kind=kOutput, calls=%fused_computation.36 | convolution fusion | flops 12892239872 | bytes 31473664 | tf_op jit(solution)/shard_map/dot_general | solution.py:34
  508.9 16.2 %convolution_add_fusion = f32[512,6144]{1,0:T(8,128)} fusion(f32[512,6144]{1,0:T(8,128)} %collective-permute-done.3, bf16[1024,6144]{1,0:T(8,128)(2,1)} %get-tuple-element.58, bf16[1024,1024]{1,0:T(8,128)(2,1)S(1)} %fusion.34), kind=kOutput, calls=%fused_computation.8 | convolution fusion | flops 6445596672 | bytes 38797312 | tf_op jit(solution)/shard_map/dot_general | solution.py:38
  553.0 33.6 %attn_bwd.2 = (bf16[1024,4096]{1,0:T(8,128)(2,1)}, f32[8,128]{1,0:T(8,128)}, f32[8,128]{1,0:T(8,128)}) custom-call(bf16[1024,4096]{1,0:T(8,128)(2,1)} %convolution_convert_fusion.qkv_ref, bf16[1024,2048]{1,0:T(8,128)(2,1)} %convolution_convert_fusion.1.do_ref, f32[1024,128]{1,0:T(8,128)} %get-tuple-element.125.cos_ref, ...), custom_call_target="tpu_custom_call" | custom-call | flops 24999999488 | bytes 14000000 | tf_op jit(solution)/shard_map/attn_bwd/pallas_call | solution.py:165
  598.9 33.6 %attn_bwd.3 = (bf16[1024,4096]{1,0:T(8,128)(2,1)}, f32[8,128]{1,0:T(8,128)}, f32[8,128]{1,0:T(8,128)}) custom-call(bf16[1024,4096]{1,0:T(8,128)(2,1)} %convolution_convert_fusion.qkv_ref, bf16[1024,2048]{1,0:T(8,128)(2,1)} %convolution_convert_fusion.1.do_ref, f32[1024,128]{1,0:T(8,128)} %get-tuple-element.125.cos_ref, ...), custom_call_target="tpu_custom_call", output_to_operand_aliasing={{0}: (6, {})} | custom-call | flops 24999999488 | bytes 14000000 | tf_op jit(solution)/shard_map/attn_bwd/pallas_call | solution.py:165
  654.0 14.6 %collective-permute-done.5 = f32[576,4096]{1,0:T(8,128)S(1)} collective-permute-done((f32[576,4096]{1,0:T(8,128)S(1)}, f32[576,4096]{1,0:T(8,128)S(1)}, u32[]{:S(2)}, u32[]{:S(2)}) %collective-permute-start.5) | collective-permute-done | bytes 9437216 | tf_op jit(solution)/shard_map/ppermute | solution.py:229
  692.9 14.0 %all-gather.3 = f32[16,1,2304]{2,1,0:T(1,128)S(1)} all-gather(f32[1,1,2304]{2,1,0:T(1,128)S(1)} %reshape.515), channel_id=3, replica_groups=mesh['fsdp'=16] {'fsdp'}, dimensions={0}, use_global_device_ids=true | all-gather | bytes 156672 | tf_op jit(solution)/shard_map/all_gather | solution.py:361
  713.2 206.0 %reduce-scatter.11.cloned.1.call-done = f32[72,4096]{1,0:T(8,128)} async-done(((f32[576,4096]{1,0:T(8,128)}), f32[72,4096]{1,0:T(8,128)}) %reduce-scatter.11.cloned.1.call-update) | async-done | bytes 1179664 | tf_op jit(solution)/shard_map/reduce_scatter | solution.py:226
  925.6 88.2 %scatter_custom_fusion = f32[9504,1024]{1,0:T(8,128)} fusion(s32[8192]{0:T(1024)S(1)} %bitcast.117, f32[8192,1024]{1,0:T(8,128)} %all-gather.19.cloned.1.call-done, f32[]{:T(128)} %constant.73.clone.1), kind=kCustom, calls=%fused_computation.6 | custom fusion | flops 8388608 | bytes 38928896 | tf_op jit(solution)/shard_map/scatter-add | solution.py:369
  1013.8 97.3 %scatter_fusion = f32[9504,1024]{1,0:T(8,128)} fusion(f32[9504,1024]{1,0:T(8,128)} %scatter_custom_fusion, s32[8192]{0:T(1024)S(1)} %bitcast.112, f32[8192,1024]{1,0:T(8,128)} %all-gather.21.cloned.1.call-done), kind=kCustom, calls=%fused_computation.5 | custom fusion | flops 8388608 | bytes 100696064 | tf_op jit(solution)/shard_map/scatter-add | solution.py:369
  (219 shorter events, 175.7 us)
Async XLA Ops:
  8.0 168.3 %reduce-scatter.7.cloned.1.call-start = ((), (), s32[]{:S(2)}) async-start(), calls=%async_computation.6 | async-start | bytes 9732096 | tf_op jit(solution)/shard_map/reduce_scatter | solution.py:226
  31.0 68.5 %copy-start.14 = (s32[8,2,2,512]{3,2,1,0:T(2,128)}, s32[8,2,2,512]{3,2,1,0:T(2,128)S(1)}, u32[]{:S(2)}) copy-start(s32[8,2,2,512]{3,2,1,0:T(2,128)S(1)} %reshape.438) | copy-start | bytes 196612
  59.7 29.3 %collective-permute-start = (bf16[4224,1024]{1,0:T(8,128)(2,1)}, bf16[4224,1024]{1,0:T(8,128)(2,1)}, u32[]{:S(2)}, u32[]{:S(2)}) collective-permute-start(bf16[4224,1024]{1,0:T(8,128)(2,1)} %gather_fusion.1), channel_id=1, source_target_pairs={{0,1},{1,0},{2,3},{3,2},{4,5},{5,4},{6,7},{7,6},{8,9},{9,8},{10,11... | collective-permute-start | bytes 25952264 | tf_op jit(solution)/shard_map/ppermute | solution.py:229
  99.2 116.0 %all-gather.17.cloned.1.call-start = ((), (), s32[]{:S(2)}) async-start(), calls=%async_computation.11 | async-start | bytes 6684672 | tf_op jit(solution)/shard_map/all_gather | solution.py:223
  128.9 29.6 %collective-permute-start.1 = (bf16[4224,1024]{1,0:T(8,128)(2,1)}, bf16[4224,1024]{1,0:T(8,128)(2,1)}, u32[]{:S(2)}, u32[]{:S(2)}) collective-permute-start(bf16[4224,1024]{1,0:T(8,128)(2,1)} %gather_fusion.3), channel_id=1, source_target_pairs={{0,1},{1,0},{2,3},{3,2},{4,5},{5,4},{6,7},{7,6},{8,9},{9,8},{10,11... | collective-permute-start | bytes 25952264 | tf_op jit(solution)/shard_map/ppermute | solution.py:229
  169.6 127.3 %reduce-scatter.9.cloned.1.call-start = ((), (), s32[]{:S(2)}) async-start(), calls=%async_computation.7 | async-start | bytes 9732096 | tf_op jit(solution)/shard_map/reduce_scatter | solution.py:226
  170.4 44.8 %copy-start.8 = (bf16[2,512,1024]{2,1,0:T(8,128)(2,1)S(1)}, bf16[2,512,1024]{2,1,0:T(8,128)(2,1)}, u32[]{:S(2)}) copy-start(bf16[2,512,1024]{2,1,0:T(8,128)(2,1)} %param.29) | copy-start | bytes 6291460
  170.4 128.3 %all-gather.11.cloned.1.call-start = ((), (), s32[]{:S(2)}) async-start(), calls=%async_computation.8 | async-start | bytes 8912896 | tf_op jit(solution)/shard_map/all_gather | solution.py:223
  171.0 191.8 %all-gather.13.cloned.1.call-start = ((), (), s32[]{:S(2)}) async-start(), calls=%async_computation.9 | async-start | bytes 4456448 | tf_op jit(solution)/shard_map/all_gather | solution.py:223
  171.6 215.5 %all-gather.15.cloned.1.call-start = ((), (), s32[]{:S(2)}) async-start(), calls=%async_computation.10 | async-start | bytes 13369344 | tf_op jit(solution)/shard_map/all_gather | solution.py:223
  172.3 535.8 %reduce-scatter.13.cloned.1.call-start = ((), (), s32[]{:S(2)}) async-start(), calls=%async_computation.15 | async-start | bytes 5308416 | tf_op jit(solution)/shard_map/reduce_scatter | solution.py:226
  172.6 126.1 %copy-start.17 = (f32[1024]{0:T(1024)}, f32[1024]{0:T(1024)S(1)}, u32[]{:S(2)}) copy-start(f32[1024]{0:T(1024)S(1)} %mul.184) | copy-start | bytes 12292
  177.7 185.1 %copy-start.4 = (bf16[512,1024]{1,0:T(8,128)(2,1)}, bf16[512,1024]{1,0:T(8,128)(2,1)S(1)}, u32[]{:S(2)}) copy-start(bf16[512,1024]{1,0:T(8,128)(2,1)S(1)} %slice.141) | copy-start | bytes 3145732
  298.2 64.6 %copy-start.6 = (bf16[512,1024]{1,0:T(8,128)(2,1)}, bf16[512,1024]{1,0:T(8,128)(2,1)S(1)}, u32[]{:S(2)}) copy-start(bf16[512,1024]{1,0:T(8,128)(2,1)S(1)} %slice.143) | copy-start | bytes 3145732
  409.0 22.9 %copy-start.9 = (bf16[2,512,1024]{2,1,0:T(8,128)(2,1)S(1)}, bf16[2,512,1024]{2,1,0:T(8,128)(2,1)}, u32[]{:S(2)}) copy-start(bf16[2,512,1024]{2,1,0:T(8,128)(2,1)} %param.29) | copy-start | bytes 6291460
  456.4 19.0 %collective-permute-start.2 = (f32[1536,1024]{1,0:T(8,128)}, f32[1536,1024]{1,0:T(8,128)}, u32[]{:S(2)}, u32[]{:S(2)}) collective-permute-start(f32[1536,1024]{1,0:T(8,128)} %bitcast.12), channel_id=1, source_target_pairs={{0,1},{1,0},{2,3},{3,2},{4,5},{5,4},{6,7},{7,6},{8,9},{9,8},{10,11... | collective-permute-start | bytes 18874376 | tf_op jit(solution)/shard_map/ppermute | solution.py:229
  482.3 26.6 %collective-permute-start.3 = (f32[512,6144]{1,0:T(8,128)}, f32[512,6144]{1,0:T(8,128)}, u32[]{:S(2)}, u32[]{:S(2)}) collective-permute-start(f32[512,6144]{1,0:T(8,128)} %fusion.39), channel_id=1, source_target_pairs={{0,1},{1,0},{2,3},{3,2},{4,5},{5,4},{6,7},{7,6},{8,9},{9,8},{10,11... | collective-permute-start | bytes 37748744 | tf_op jit(solution)/shard_map/ppermute | solution.py:229
  530.4 7.9 collective-permute-start.4
  543.6 166.9 %reduce-scatter.15.cloned.1.call-start = ((), (), s32[]{:S(2)}) async-start(), calls=%async_computation.16 | async-start | bytes 14155776 | tf_op jit(solution)/shard_map/reduce_scatter | solution.py:226
  544.2 375.0 %reduce-scatter.11.cloned.1.call-start = ((), (), s32[]{:S(2)}) async-start(), calls=%async_computation.14 | async-start | bytes 10616832 | tf_op jit(solution)/shard_map/reduce_scatter | solution.py:226
  653.9 14.7 %collective-permute-start.5 = (f32[576,4096]{1,0:T(8,128)S(1)}, f32[576,4096]{1,0:T(8,128)S(1)}, u32[]{:S(2)}, u32[]{:S(2)}) collective-permute-start(f32[576,4096]{1,0:T(8,128)S(1)} %fusion.35), channel_id=1, source_target_pairs={{0,1},{1,0},{2,3},{3,2},{4,5},{5,4},{6,7},{7,6},{8,9},{9,8},{10,11... | collective-permute-start | bytes 28311560 | tf_op jit(solution)/shard_map/ppermute | solution.py:229
  678.5 247.2 %all-gather.19.cloned.1.call-start = ((), (), s32[]{:S(2)}) async-start(), calls=%async_computation.12 | async-start | bytes 35651584 | tf_op jit(solution)/shard_map/all_gather | solution.py:223
  679.2 334.6 %all-gather.21.cloned.1.call-start = ((), (), s32[]{:S(2)}) async-start(), calls=%async_computation.13 | async-start | bytes 35651584 | tf_op jit(solution)/shard_map/all_gather | solution.py:223
  680.0 431.2 %reduce-scatter.17.cloned.1.call-start = ((), (), s32[]{:S(2)}) async-start(), calls=%async_computation.17 | async-start | bytes 7077888 | tf_op jit(solution)/shard_map/reduce_scatter | solution.py:226
  (28 other events, 244.9 us)
Sparse Core Ops, SparseCore 0:
  99.3 76.9 reduce-scatter.6
  181.2 115.6 reduce-scatter.8
  543.7 52.2 reduce-scatter.12
  600.4 102.8 reduce-scatter.14
  707.3 211.8 reduce-scatter.10
  923.5 108.3 reduce-scatter.16
Sparse Core Ops, SparseCore 1:
  169.7 45.5 all-gather.16
  217.9 58.9 all-gather.10
  279.0 42.6 all-gather.12
  324.4 62.5 all-gather.14
  681.5 151.3 all-gather.18
  835.1 146.2 all-gather.20

commit v2 on v1

--- a/solution.py
+++ b/solution.py
@@ -72,19 +72,19 @@
     cos_t, sin_t = cos_ref[...], sin_ref[...]
     k_n, _ = norm_fwd(qkv_ref[:, n_rep * hd:(n_rep + 1) * hd])
     k_rot = rope(k_n * kg_ref[...], cos_t, sin_t).astype(jnp.bfloat16)
-    v_raw = qkv_ref[:, (n_rep + 1) * hd:(n_rep + 2) * hd]
+    v_t = qkv_ref[:, (n_rep + 1) * hd:(n_rep + 2) * hd].astype(jnp.float32).T.astype(jnp.bfloat16)
     for rep in range(n_rep):
         q_n, _ = norm_fwd(qkv_ref[:, rep * hd:(rep + 1) * hd])
         q_rot = rope(q_n * qg_ref[...], cos_t, sin_t).astype(jnp.bfloat16)
         for lo in range(0, seq, chunk):
             end = lo + chunk
-            s = kdot_nt(q_rot[lo:end], k_rot[:end]) * scale
-            rows = lax.broadcasted_iota(jnp.int32, s.shape, 0) + lo
-            cols = lax.broadcasted_iota(jnp.int32, s.shape, 1)
-            s = jnp.where(rows >= cols, s, NEG)
-            e = jnp.exp(s - jnp.max(s, axis=-1, keepdims=True))
-            p = e * (1.0 / jnp.sum(e, axis=-1, keepdims=True))
-            o = kdot_nn(p.astype(jnp.bfloat16), v_raw[:end])
+            s = kdot_nt(k_rot[:end], q_rot[lo:end]) * scale
+            keys = lax.broadcasted_iota(jnp.int32, s.shape, 0)
+            qpos = lax.broadcasted_iota(jnp.int32, s.shape, 1) + lo
+            s = jnp.where(qpos >= keys, s, NEG)
+            e = jnp.exp(s - jnp.max(s, axis=0, keepdims=True))
+            p = e * (1.0 / jnp.sum(e, axis=0, keepdims=True))
+            o = kdot_nn(v_t[:, :end], p.astype(jnp.bfloat16)).T
             out_ref[lo:end, rep * hd:(rep + 1) * hd] = o.astype(jnp.bfloat16)
             rep_refs[rep][lo:end] = o.astype(jnp.bfloat16)
 
@@ -184,14 +184,35 @@
     )(qkv, do, cos_t, sin_t, q_gain, k_gain, *prev)
 
 
-def mlp_bwd_kernel(ff, gu_ref, ga_ref, out_ref, act_ref, act_t_ref):
+def mlp_act_kernel(ff, n_chip, core_ref, gu_ref, act_ref, act_t_ref):
+    gate, up = gu_ref[:, :ff], gu_ref[:, ff:]
+    act = gate * jax.nn.sigmoid(gate) * up
+    act_ref[...] = act.astype(jnp.bfloat16)
+    act_t = act.T.astype(jnp.bfloat16)
+    block = ff // (2 * n_chip)
+    for i in range(2 * n_chip):
+        act_t_ref[lax.bitwise_xor(core_ref[0], i % 2), i // 2] = act_t[i * block:(i + 1) * block]
+
+
+def mlp_act(gu, core, n_chip):
+    tokens, ff = gu.shape[0], gu.shape[1] // 2
+    rows = 128
+    return pl.pallas_call(
+        functools.partial(mlp_act_kernel, ff, n_chip),
+        grid=(tokens // rows,),
+        in_specs=[pl.BlockSpec(memory_space=pltpu.SMEM), pl.BlockSpec((rows, 2 * ff), lambda i: (i, 0))],
+        out_specs=[pl.BlockSpec((rows, ff), lambda i: (i, 0)), pl.BlockSpec((2, n_chip, ff // (2 * n_chip), rows), lambda i: (0, 0, 0, i))],
+        out_shape=[jax.ShapeDtypeStruct((tokens, ff), jnp.bfloat16), jax.ShapeDtypeStruct((2, n_chip, ff // (2 * n_chip), tokens), jnp.bfloat16)],
+        cost_estimate=pl.CostEstimate(flops=12_000_000_000, bytes_accessed=38_000_000, transcendentals=3_200_000),
+        name='mlp_act',
+    )(core.reshape(1), gu)
+
+
+def mlp_bwd_kernel(ff, gu_ref, ga_ref, out_ref):
     gate, up, grad_act = gu_ref[:, :ff], gu_ref[:, ff:], ga_ref[...]
     sig = jax.nn.sigmoid(gate)
     out_ref[:, :ff] = (grad_act * up * sig * (1.0 + gate * (1.0 - sig))).astype(jnp.bfloat16)
     out_ref[:, ff:] = (grad_act * gate * sig).astype(jnp.bfloat16)
-    act = gate * sig * up
-    act_ref[...] = act.astype(jnp.bfloat16)
-    act_t_ref[...] = act.T.astype(jnp.bfloat16)
 
 
 def mlp_bwd(gu, grad_act):
@@ -201,8 +222,8 @@
         functools.partial(mlp_bwd_kernel, ff),
         grid=(tokens // rows,),
         in_specs=[pl.BlockSpec((rows, 2 * ff), lambda i: (i, 0)), pl.BlockSpec((rows, ff), lambda i: (i, 0))],
-        out_specs=[pl.BlockSpec((rows, 2 * ff), lambda i: (i, 0)), pl.BlockSpec((rows, ff), lambda i: (i, 0)), pl.BlockSpec((ff, rows), lambda i: (0, i))],
-        out_shape=[jax.ShapeDtypeStruct((tokens, 2 * ff), jnp.bfloat16), jax.ShapeDtypeStruct((tokens, ff), jnp.bfloat16), jax.ShapeDtypeStruct((ff, tokens), jnp.bfloat16)],
+        out_specs=pl.BlockSpec((rows, 2 * ff), lambda i: (i, 0)),
+        out_shape=jax.ShapeDtypeStruct((tokens, 2 * ff), jnp.bfloat16),
         cost_estimate=pl.CostEstimate(flops=16_000_000_000, bytes_accessed=50_000_000, transcendentals=3_200_000),
         name='mlp_bwd',
     )(gu, grad_act)
@@ -271,9 +292,10 @@
             ids = jnp.pad(all_ids[:, :, b], ((0, 0), (0, 0), (0, seq_pad - seq)), constant_values=-1)
             near, far = near_far(ids, 1)
             near, far = near.reshape(-1), far.reshape(-1)
-            recv = swap_core(pick(far))
+            near_rows, far_rows = pick(near), pick(far)
+            recv = swap_core(far_rows)
             zero = jnp.zeros((), table_shard.dtype)
-            merged = jnp.where(local_rows(near, me)[1], pick(near), jnp.where(local_rows(near, me + 1 - 2 * core)[1], recv, zero))
+            merged = jnp.where(local_rows(near, me)[1], near_rows, jnp.where(local_rows(near, me + 1 - 2 * core)[1], recv, zero))
             return merged
 
         wo = gather(w_out)
@@ -299,9 +321,14 @@
         mlp_in = (normed2 * mlp_gain).astype(jnp.bfloat16)
         gu = dot_nn(mlp_in, wgu)
 
+        act, act_t = mlp_act(gu, core, n_chip)
+
         dy = dy_out.reshape(n_tok, dim)
-        grad_act = dot_nt(dy, wdown)
-        dgu, act, act_t = mlp_bwd(gu, grad_act)
+        part_down = kdot_nn(act_t[0].reshape(-1, n_tok), dy) + swap_core(kdot_nn(act_t[1].reshape(-1, n_tok), dy))
+        dy_b, part_down = lax.optimization_barrier((dy, part_down))
+        g_down = scatter_chips(part_down)
+        grad_act = dot_nt(dy_b, wdown)
+        dgu = mlp_bwd(gu, grad_act)
 
         row_ids = jnp.arange(dim)
 
@@ -314,10 +341,7 @@
             return both[:, :n_chip * block], both[:, n_chip * block:]
 
         near2, far2 = split_cores(mlp_in, shard_rows)
-        near_down, far_down = near_far(kdot_nn(act_t, dy).reshape(n_chip, 2, -1, dim), 1)
-        part_down = near_down.reshape(-1, dim) + swap_core(far_down.reshape(-1, dim))
-        far_gu, part_down, dgu = lax.optimization_barrier((dot_tn(far2, dgu), part_down, dgu))
-        g_down = scatter_chips(part_down)
+        far_gu, dgu = lax.optimization_barrier((dot_tn(far2, dgu), dgu))
         recv_gu = swap_core(far_gu)
         grad_mlp_in = dot_nt(dgu, wgu)
         part_gu = dot_tn(near2, dgu) + recv_gu
@@ -333,7 +357,6 @@
         recv_out = swap_core(dot_tn(far_h, hidden_pad))
         grad_heads = dot_nt(hidden_b, wo).astype(jnp.bfloat16)
         part_out = dot_tn(near_h, hidden_pad) + recv_out
-        grad_heads, part_out = lax.optimization_barrier((grad_heads, part_out))
         g_out = scatter_chips(part_out)[:, :dim]
         local_ids = (all_ids - me * rows_local).reshape(n_dev, batch, seq)
         slots = jnp.where((local_ids >= 0) & (local_ids < rows_local), local_ids, rows_local)
@@ -352,7 +375,8 @@
             dqkv = (dqkv,)
         dqkv, = dqkv
         near1, far1 = split_cores(attn_in, -(-shard_rows // 24) * 24)
-        part_qkv = dot_tn(near1, dqkv) + swap_core(dot_tn(far1, dqkv))
+        far_qkv = dot_tn(far1, dqkv)
+        part_qkv = dot_tn(near1, dqkv) + swap_core(far_qkv)
         g_qkv = scatter_chips(part_qkv)[:shard_rows]
         layer_out = (hidden.astype(jnp.float32) + dot_nn(act, wdown)).astype(jnp.bfloat16)
 

time: 1130 us -> 1100 us (0.973)
    all_gather x6, waiting for transfers between devices: 52.5 us -> 0.06 us  [gather(): return lax.all_gather(shard, AXIS_NAME, tiled=True)]
    reduce_scatter x6, waiting for transfers between devices: 275 us -> 307 us  [scatter_chips(): lax.psum_scatter(part, AXIS_NAME, scatter_dimension=0, tiled=True, axis_i...]
    pallas_call x0 -> x1, Pallas kernels: none -> 15.5 us  [mlp_act(): pl.pallas_call(functools.partial(mlp_act_kernel, ff, n_chip), grid=(token...]
    pallas_call x1, Pallas kernels: 48.5 us -> 34.7 us  [attn_fwd(): pl.pallas_call(functools.partial(attn_fwd_kernel, n_rep, hd, seq // 2), g...]
    dynamic_slice x3 -> x2, local copies, waits for them, and re-layouts: 12 us -> 0.07 us  [near_far(): lax.dynamic_index_in_dim(blocks, core, axis, False)]
    ppermute x6, waiting for transfers between devices: 16.1 us -> 27.8 us  [swap_core(): return lax.ppermute(part, AXIS_NAME, pairs)]
  transfers between devices with their start and end apart: 18 -> 18, of which waited for: 6 -> 6; matrix products, arithmetic and copies ran while one was open for 41% -> 43% of each run, Pallas kernels for 10% -> 11%
where the time goes in v2:
time: 1100 us; the launch traced here: 1090 us
  waiting for transfers between devices  339 us (31%)
  other arithmetic  224 us (20%)
  matrix products  199 us (18%)
  local copies, waits for them, and re-layouts  147 us (13%)
  Pallas kernels  136 us (12%)
  blocking collectives  29.2 us (3%)
  between operations  16.8 us (2%)
    reduce_scatter x6, waiting for transfers between devices, scatter_chips(): lax.psum_scatter(part, AXIS_NAME, scatter_dimension=0, tiled=True, axis_i...  307 us
    scatter-add x2, other arithmetic, device_step(): d_table = d_table.at[slots[:, b].reshape(-1)].add(all_rows[b], mode='drop')  185 us
    gather x4, local copies, waits for them, and re-layouts, pick(): jnp.take(table_shard, jnp.clip(local, 0, rows_local - 1), axis=0, mode='c...  116 us
    dot_general x6, matrix products, dot_nn(): lax.dot_general(split_rows(a), b, (((2,), (0,)), ((), ())), preferred_ele...  69.8 us
    pallas_call x2, Pallas kernels, attn_bwd(): pl.pallas_call(functools.partial(attn_bwd_kernel, n_rep, hd, seq // 2, le...  67.6 us
    dot_general x5, matrix products, dot_nt(): lax.dot_general(split_rows(a), b, (((2,), (1,)), ((), ())), preferred_ele...  61.7 us
    dot_general x6, matrix products, dot_tn(): lax.dot_general(split_rows(a), split_rows(b), (((0, 1), (0, 1)), ((), ())...  55 us
    pallas_call x1, Pallas kernels, attn_fwd(): pl.pallas_call(functools.partial(attn_fwd_kernel, n_rep, hd, seq // 2), g...  34.7 us
  transfers between devices with their start and end apart: 18, of which 6 were waited for; matrix products, arithmetic and copies ran while one was open for 43% of the time, Pallas kernels for 11%

profile of v2, /device:TPU:0, one launch (start us, length us, event | category | flops | bytes accessed | tf_op | source)
XLA Modules:
  0.0 1094.0 jit_solution(8584184549261211141)
XLA Ops:
  10.2 14.8 %all-gather.2 = f32[16,1,1152]{2,1,0:T(1,128)S(1)} all-gather(f32[1,1,1152]{2,1,0:T(1,128)S(1)} %reshape.505), channel_id=2, replica_groups=mesh['fsdp'=16] {'fsdp'}, dimensions={0}, use_global_device_ids=true | all-gather | bytes 78336 | tf_op jit(solution)/shard_map/all_gather | solution.py:268
  31.2 28.6 %gather_fusion.1 = bf16[4224,1024]{1,0:T(8,128)(2,1)} fusion(bf16[9504,1024]{1,0:T(8,128)(2,1)} %param.17, s32[5120]{0:T(1024)S(1)} %pad_clamp_fusion.2), kind=kCustom, calls=%fused_computation.1 | custom fusion | bytes 17318400 | tf_op jit(solution)/shard_map/jit(_take)/gather | solution.py:287
  60.4 28.6 %gather_fusion = bf16[4224,1024]{1,0:T(8,128)(2,1)} fusion(bf16[9504,1024]{1,0:T(8,128)(2,1)} %param.17, s32[5120]{0:T(1024)S(1)} %pad_clamp_fusion.3), kind=kCustom, calls=%fused_computation | custom fusion | bytes 17318400 | tf_op jit(solution)/shard_map/jit(_take)/gather | solution.py:287
  99.7 29.3 %gather_fusion.3 = bf16[4224,1024]{1,0:T(8,128)(2,1)} fusion(bf16[9504,1024]{1,0:T(8,128)(2,1)} %param.17, s32[5120]{0:T(1024)S(1)} %pad_clamp_fusion), kind=kCustom, calls=%fused_computation.3 | custom fusion | bytes 17318400 | tf_op jit(solution)/shard_map/jit(_take)/gather | solution.py:287
  129.5 29.1 %gather_fusion.2 = bf16[4224,1024]{1,0:T(8,128)(2,1)} fusion(bf16[9504,1024]{1,0:T(8,128)(2,1)} %param.17, s32[5120]{0:T(1024)S(1)} %pad_clamp_fusion.1), kind=kCustom, calls=%fused_computation.2 | custom fusion | bytes 17318400 | tf_op jit(solution)/shard_map/jit(_take)/gather | solution.py:287
  158.6 11.0 %select_select_fusion = bf16[4224,1024]{1,0:T(8,128)(2,1)} fusion(bf16[4224,1024]{1,0:T(8,128)(2,1)} %gather_fusion.2, bf16[4224,1024]{1,0:T(8,128)(2,1)} %collective-permute-done.1, pred[4224]{0:T(1024)(128)(4,1)S(1)} %and.52, pred[4224]{0:T(1024)(128)(4,1)S(1)} %and.50), kind=kLoop, calls=%fused_computation.9 | loop fusion | flops 8650752 | bytes 25960704 | tf_op jit(solution)/shard_map/jit(_where)/select_n | solution.py:298
  177.7 107.2 %reduce-scatter.9.cloned.1.call-done = bf16[528,1024]{1,0:T(8,128)(2,1)} async-done(((bf16[4224,1024]{1,0:T(8,128)(2,1)}), bf16[528,1024]{1,0:T(8,128)(2,1)}) %reduce-scatter.9.cloned.1.call-update) | async-done | bytes 1081360 | tf_op jit(solution)/shard_map/reduce_scatter | solution.py:247
  286.9 15.8 %convolution_convert_fusion.qkv_ref = bf16[1024,4096]{1,0:T(8,128)(2,1)} fusion(bf16[1024,4096]{1,0:T(8,128)(2,1)} %all-gather.11.cloned.1.call-done, f32[1024]{0:T(1024)S(1)} %mul.184, f32[1024]{0:T(1024)S(1)} %add_rsqrt_fusion.1, bf16[512,1024]{1,0:T(8,128)(2,1)S(1)} %slice.151, bf16[512,1024]{1,0:T(8,128)(2,1)S(1)} %slice.149), kind=kOutput, calls=%fused_computation.11 | convolution fusion | flops 8601468928 | bytes 18882560 | tf_op jit(solution)/shard_map/dot_general | solution.py:30
  302.7 34.7 %attn_fwd.1 = (bf16[1024,2048]{1,0:T(8,128)(2,1)}, bf16[1024,1024]{1,0:T(8,128)(2,1)}, bf16[1024,1024]{1,0:T(8,128)(2,1)}) custom-call(bf16[1024,4096]{1,0:T(8,128)(2,1)} %convolution_convert_fusion.qkv_ref, f32[1024,128]{1,0:T(8,128)} %get-tuple-element.121.cos_ref, f32[1024,128]{1,0:T(8,128)} %get-tuple-element.122.sin_ref, ...), custom_call_target="tpu_custom_call" | custom-call | flops 24999999488 | bytes 14000000 | tf_op jit(solution)/shard_map/attn_fwd/pallas_call | solution.py:96
  346.9 21.7 %fusion.39.gu_ref = f32[1024,6144]{1,0:T(8,128)} fusion(bf16[1024,6144]{1,0:T(8,128)(2,1)} %all-gather.15.cloned.1.call-done, bf16[1024,1024]{1,0:T(8,128)(2,1)} %get-tuple-element.117, f32[1024]{0:T(1024)S(1)} %mul.196, f32[1024]{0:T(1024)S(1)} %add_rsqrt_fusion), kind=kOutput, calls=%fused_computation.72 | convolution fusion | flops 12889096192 | bytes 39854080 | tf_op jit(solution)/shard_map/dot_general | solution.py:30
  368.5 15.5 %mlp_act.1 = (bf16[1024,3072]{1,0:T(8,128)(2,1)}, bf16[2,8,192,1024]{3,2,1,0:T(8,128)(2,1)}) custom-call(s32[1]{0:T(128)} %bitcast.5.core_ref, f32[1024,6144]{1,0:T(8,128)} %fusion.39.gu_ref), custom_call_target="tpu_custom_call" | custom-call | flops 12000000000 | bytes 38000000 | tf_op jit(solution)/shard_map/mlp_act/pallas_call | solution.py:200
  413.0 12.1 %fusion.61.ga_ref = f32[1024,3072]{1,0:T(8,128)} fusion(bf16[1024,1024]{1,0:T(8,128)(2,1)} %bitcast.91, bf16[3072,1024]{1,0:T(8,128)(2,1)} %all-gather.17.cloned.1.call-done), kind=kOutput, calls=%fused_computation.138 | convolution fusion | flops 6442450944 | bytes 20971520 | tf_op jit(solution)/shard_map/dot_general | solution.py:34
  425.1 18.2 %mlp_bwd.1 = bf16[1024,6144]{1,0:T(8,128)(2,1)} custom-call(f32[1024,6144]{1,0:T(8,128)} %fusion.39.gu_ref, f32[1024,3072]{1,0:T(8,128)} %fusion.61.ga_ref), custom_call_target="tpu_custom_call" | custom-call | flops 16000000000 | bytes 50000000 | tf_op jit(solution)/shard_map/mlp_bwd/pallas_call | solution.py:221
  443.4 14.5 %fusion.37 = f32[512,6144]{1,0:T(8,128)} fusion(bf16[1024,6144]{1,0:T(8,128)(2,1)} %mlp_bwd.1, bf16[1024,1024]{1,0:T(8,128)(2,1)S(1)} %fusion.32), kind=kOutput, calls=%fused_computation.67 | convolution fusion | flops 6442450944 | bytes 26214400 | tf_op jit(solution)/shard_map/dot_general | solution.py:38
  458.0 22.3 %fusion.14 = (f32[1024]{0:T(1024)}, f32[1024]{0:T(1024)S(1)}, f32[1024,1024]{1,0:T(8,128)S(1)}) fusion(bf16[1024,1024]{1,0:T(8,128)(2,1)} %get-tuple-element.117, f32[1024]{0:T(1024)S(1)} %add_rsqrt_fusion, f32[1024]{0:T(1024)S(1)} %mul.196, bf16[1024,6144]{1,0:T(8,128)(2,1)} %mlp_bwd.1, bf16[1024,6144]{1,0:T(8,128)(2,1)} %all-gather.15.cloned.1.call-done), kind=kOutput, calls=%fused_computation.34 | convolution fusion | flops 12892239872 | bytes 31473664 | tf_op jit(solution)/shard_map/dot_general | solution.py:34
  487.2 12.7 %convolution_add_fusion = f32[512,6144]{1,0:T(8,128)} fusion(f32[512,6144]{1,0:T(8,128)} %collective-permute-done.3, bf16[1024,6144]{1,0:T(8,128)(2,1)S(1)} %copy-done, bf16[1024,1024]{1,0:T(8,128)(2,1)} %copy-done.9), kind=kOutput, calls=%fused_computation.8 | convolution fusion | flops 6445596672 | bytes 38797312 | tf_op jit(solution)/shard_map/dot_general | solution.py:38
  534.2 33.5 %attn_bwd.2 = (bf16[1024,4096]{1,0:T(8,128)(2,1)}, f32[8,128]{1,0:T(8,128)}, f32[8,128]{1,0:T(8,128)}) custom-call(bf16[1024,4096]{1,0:T(8,128)(2,1)} %convolution_convert_fusion.qkv_ref, bf16[1024,2048]{1,0:T(8,128)(2,1)} %convolution_convert_fusion.1.do_ref, f32[1024,128]{1,0:T(8,128)} %get-tuple-element.121.cos_ref, ...), custom_call_target="tpu_custom_call" | custom-call | flops 24999999488 | bytes 14000000 | tf_op jit(solution)/shard_map/attn_bwd/pallas_call | solution.py:165
  579.7 34.0 %attn_bwd.3 = (bf16[1024,4096]{1,0:T(8,128)(2,1)}, f32[8,128]{1,0:T(8,128)}, f32[8,128]{1,0:T(8,128)}) custom-call(bf16[1024,4096]{1,0:T(8,128)(2,1)} %convolution_convert_fusion.qkv_ref, bf16[1024,2048]{1,0:T(8,128)(2,1)} %convolution_convert_fusion.1.do_ref, f32[1024,128]{1,0:T(8,128)} %get-tuple-element.121.cos_ref, ...), custom_call_target="tpu_custom_call", output_to_operand_aliasing={{0}: (6, {})} | custom-call | flops 24999999488 | bytes 14000000 | tf_op jit(solution)/shard_map/attn_bwd/pallas_call | solution.py:165
  635.4 14.3 %collective-permute-done.4 = f32[576,4096]{1,0:T(8,128)S(1)} collective-permute-done((f32[576,4096]{1,0:T(8,128)S(1)}, f32[576,4096]{1,0:T(8,128)S(1)}, u32[]{:S(2)}, u32[]{:S(2)}) %collective-permute-start.4) | collective-permute-done | bytes 9437216 | tf_op jit(solution)/shard_map/ppermute | solution.py:250
  661.9 12.5 %fusion.16 = bf16[1024,1024]{1,0:T(8,128)(2,1)} fusion(bf16[1024,1024]{1,0:T(8,128)(2,1)S(1)} %copy-done.15, bf16[1024,3072]{1,0:T(8,128)(2,1)} %get-tuple-element.67, bf16[3072,1024]{1,0:T(8,128)(2,1)} %all-gather.17.cloned.1.call-done), kind=kOutput, calls=%fused_computation.36 | convolution fusion | flops 6445596672 | bytes 16777216 | tf_op jit(solution)/shard_map/dot_general | solution.py:30
  674.6 14.4 %all-gather.3 = f32[16,1,2304]{2,1,0:T(1,128)S(1)} all-gather(f32[1,1,2304]{2,1,0:T(1,128)S(1)} %reshape.507), channel_id=3, replica_groups=mesh['fsdp'=16] {'fsdp'}, dimensions={0}, use_global_device_ids=true | all-gather | bytes 156672 | tf_op jit(solution)/shard_map/all_gather | solution.py:385
  695.4 198.8 %reduce-scatter.11.cloned.1.call-done = f32[72,4096]{1,0:T(8,128)} async-done(((f32[576,4096]{1,0:T(8,128)}), f32[72,4096]{1,0:T(8,128)}) %reduce-scatter.11.cloned.1.call-update) | async-done | bytes 1179664 | tf_op jit(solution)/shard_map/reduce_scatter | solution.py:247
  900.6 88.2 %scatter_custom_fusion = f32[9504,1024]{1,0:T(8,128)} fusion(s32[8192]{0:T(1024)S(1)} %bitcast.111, f32[8192,1024]{1,0:T(8,128)} %all-gather.19.cloned.1.call-done, f32[]{:T(128)} %constant.67.clone.1), kind=kCustom, calls=%fused_computation.6 | custom fusion | flops 8388608 | bytes 38928896 | tf_op jit(solution)/shard_map/scatter-add | solution.py:393
  988.9 97.3 %scatter_fusion = f32[9504,1024]{1,0:T(8,128)} fusion(f32[9504,1024]{1,0:T(8,128)} %scatter_custom_fusion, s32[8192]{0:T(1024)S(1)} %bitcast.106, f32[8192,1024]{1,0:T(8,128)} %all-gather.21.cloned.1.call-done), kind=kCustom, calls=%fused_computation.5 | custom fusion | flops 8388608 | bytes 100696064 | tf_op jit(solution)/shard_map/scatter-add | solution.py:393
  (223 shorter events, 167.9 us)
Async XLA Ops:
  8.0 168.3 %reduce-scatter.7.cloned.1.call-start = ((), (), s32[]{:S(2)}) async-start(), calls=%async_computation.6 | async-start | bytes 9732096 | tf_op jit(solution)/shard_map/reduce_scatter | solution.py:247
  31.0 68.5 %copy-start.18 = (s32[8,2,2,512]{3,2,1,0:T(2,128)}, s32[8,2,2,512]{3,2,1,0:T(2,128)S(1)}, u32[]{:S(2)}) copy-start(s32[8,2,2,512]{3,2,1,0:T(2,128)S(1)} %reshape.432) | copy-start | bytes 196612
  59.7 29.3 %collective-permute-start = (bf16[4224,1024]{1,0:T(8,128)(2,1)}, bf16[4224,1024]{1,0:T(8,128)(2,1)}, u32[]{:S(2)}, u32[]{:S(2)}) collective-permute-start(bf16[4224,1024]{1,0:T(8,128)(2,1)} %gather_fusion.1), channel_id=1, source_target_pairs={{0,1},{1,0},{2,3},{3,2},{4,5},{5,4},{6,7},{7,6},{8,9},{9,8},{10,11... | collective-permute-start | bytes 25952264 | tf_op jit(solution)/shard_map/ppermute | solution.py:250
  99.2 185.7 %reduce-scatter.9.cloned.1.call-start = ((), (), s32[]{:S(2)}) async-start(), calls=%async_computation.7 | async-start | bytes 9732096 | tf_op jit(solution)/shard_map/reduce_scatter | solution.py:247
  129.0 29.6 %collective-permute-start.1 = (bf16[4224,1024]{1,0:T(8,128)(2,1)}, bf16[4224,1024]{1,0:T(8,128)(2,1)}, u32[]{:S(2)}, u32[]{:S(2)}) collective-permute-start(bf16[4224,1024]{1,0:T(8,128)(2,1)} %gather_fusion.3), channel_id=1, source_target_pairs={{0,1},{1,0},{2,3},{3,2},{4,5},{5,4},{6,7},{7,6},{8,9},{9,8},{10,11... | collective-permute-start | bytes 25952264 | tf_op jit(solution)/shard_map/ppermute | solution.py:250
  169.6 117.3 %all-gather.11.cloned.1.call-start = ((), (), s32[]{:S(2)}) async-start(), calls=%async_computation.8 | async-start | bytes 8912896 | tf_op jit(solution)/shard_map/all_gather | solution.py:244
  170.2 167.2 %all-gather.13.cloned.1.call-start = ((), (), s32[]{:S(2)}) async-start(), calls=%async_computation.9 | async-start | bytes 4456448 | tf_op jit(solution)/shard_map/all_gather | solution.py:244
  170.8 176.1 %all-gather.15.cloned.1.call-start = ((), (), s32[]{:S(2)}) async-start(), calls=%async_computation.10 | async-start | bytes 13369344 | tf_op jit(solution)/shard_map/all_gather | solution.py:244
  171.4 241.6 %all-gather.17.cloned.1.call-start = ((), (), s32[]{:S(2)}) async-start(), calls=%async_computation.11 | async-start | bytes 6684672 | tf_op jit(solution)/shard_map/all_gather | solution.py:244
  171.7 115.2 %copy-start.21 = (f32[1024]{0:T(1024)}, f32[1024]{0:T(1024)S(1)}, u32[]{:S(2)}) copy-start(f32[1024]{0:T(1024)S(1)} %mul.184) | copy-start | bytes 12292
  175.5 515.4 %reduce-scatter.13.cloned.1.call-start = ((), (), s32[]{:S(2)}) async-start(), calls=%async_computation.15 | async-start | bytes 5308416 | tf_op jit(solution)/shard_map/reduce_scatter | solution.py:247
  177.7 159.7 %copy-start.5 = (bf16[512,1024]{1,0:T(8,128)(2,1)}, bf16[512,1024]{1,0:T(8,128)(2,1)S(1)}, u32[]{:S(2)}) copy-start(bf16[512,1024]{1,0:T(8,128)(2,1)S(1)} %slice.149) | copy-start | bytes 3145732
  286.4 51.1 %copy-start.7 = (bf16[512,1024]{1,0:T(8,128)(2,1)}, bf16[512,1024]{1,0:T(8,128)(2,1)S(1)}, u32[]{:S(2)}) copy-start(bf16[512,1024]{1,0:T(8,128)(2,1)S(1)} %slice.151) | copy-start | bytes 3145732
  395.2 10.5 collective-permute-start.2
  399.7 43.7 %copy-start.9 = (bf16[1024,1024]{1,0:T(8,128)(2,1)}, bf16[1024,1024]{1,0:T(8,128)(2,1)S(1)}, u32[]{:S(2)}) copy-start(bf16[1024,1024]{1,0:T(8,128)(2,1)S(1)} %fusion.32) | copy-start | bytes 6291460
  457.9 26.6 %collective-permute-start.3 = (f32[512,6144]{1,0:T(8,128)}, f32[512,6144]{1,0:T(8,128)}, u32[]{:S(2)}, u32[]{:S(2)}) collective-permute-start(f32[512,6144]{1,0:T(8,128)} %fusion.37), channel_id=1, source_target_pairs={{0,1},{1,0},{2,3},{3,2},{4,5},{5,4},{6,7},{7,6},{8,9},{9,8},{10,11... | collective-permute-start | bytes 37748744 | tf_op jit(solution)/shard_map/ppermute | solution.py:250
  458.0 22.4 %copy-start.14 = (bf16[1024,1024]{1,0:T(8,128)(2,1)S(1)}, bf16[1024,1024]{1,0:T(8,128)(2,1)}, u32[]{:S(2)}) copy-start(bf16[1024,1024]{1,0:T(8,128)(2,1)} %get-tuple-element.117) | copy-start | bytes 6291460
  505.2 7.9 collective-permute-start.5
  517.9 174.8 %reduce-scatter.15.cloned.1.call-start = ((), (), s32[]{:S(2)}) async-start(), calls=%async_computation.16 | async-start | bytes 14155776 | tf_op jit(solution)/shard_map/reduce_scatter | solution.py:247
  518.5 375.7 %reduce-scatter.11.cloned.1.call-start = ((), (), s32[]{:S(2)}) async-start(), calls=%async_computation.14 | async-start | bytes 10616832 | tf_op jit(solution)/shard_map/reduce_scatter | solution.py:247
  634.9 14.9 %collective-permute-start.4 = (f32[576,4096]{1,0:T(8,128)S(1)}, f32[576,4096]{1,0:T(8,128)S(1)}, u32[]{:S(2)}, u32[]{:S(2)}) collective-permute-start(f32[576,4096]{1,0:T(8,128)S(1)} %fusion.33), channel_id=1, source_target_pairs={{0,1},{1,0},{2,3},{3,2},{4,5},{5,4},{6,7},{7,6},{8,9},{9,8},{10,11... | collective-permute-start | bytes 28311560 | tf_op jit(solution)/shard_map/ppermute | solution.py:250
  659.5 241.1 %all-gather.19.cloned.1.call-start = ((), (), s32[]{:S(2)}) async-start(), calls=%async_computation.12 | async-start | bytes 35651584 | tf_op jit(solution)/shard_map/all_gather | solution.py:244
  660.3 328.6 %all-gather.21.cloned.1.call-start = ((), (), s32[]{:S(2)}) async-start(), calls=%async_computation.13 | async-start | bytes 35651584 | tf_op jit(solution)/shard_map/all_gather | solution.py:244
  661.0 425.1 %reduce-scatter.17.cloned.1.call-start = ((), (), s32[]{:S(2)}) async-start(), calls=%async_computation.17 | async-start | bytes 7077888 | tf_op jit(solution)/shard_map/reduce_scatter | solution.py:247
  (30 other events, 253.2 us)
Sparse Core Ops, SparseCore 0:
  99.3 76.9 reduce-scatter.6
  181.2 103.7 reduce-scatter.8
  518.0 52.8 reduce-scatter.12
  575.5 102.6 reduce-scatter.14
  682.1 212.0 reduce-scatter.10
  898.6 108.3 reduce-scatter.16
Sparse Core Ops, SparseCore 1:
  172.9 57.7 all-gather.10
  232.8 44.5 all-gather.12
  280.1 62.5 all-gather.14
  344.9 42.0 all-gather.16
  662.6 145.2 all-gather.18
  810.2 146.2 all-gather.20

commit v3 on v2

--- a/solution.py
+++ b/solution.py
@@ -66,7 +66,8 @@
     return values * cos_t + pltpu.roll(values, values.shape[-1] // 2, 1) * sin_t
 
 
-def attn_fwd_kernel(n_rep, hd, chunk, qkv_ref, cos_ref, sin_ref, qg_ref, kg_ref, out_ref, *rep_refs):
+def attn_fwd_kernel(n_rep, hd, chunk, n_alias, qkv_ref, cos_ref, sin_ref, qg_ref, kg_ref, *rest):
+    out_ref, *rep_refs = rest[n_alias:]
     seq = qkv_ref.shape[0]
     scale = hd ** -0.5
     cos_t, sin_t = cos_ref[...], sin_ref[...]
@@ -89,23 +90,23 @@
             rep_refs[rep][lo:end] = o.astype(jnp.bfloat16)
 
 
-def attn_fwd(qkv, cos_t, sin_t, q_gain, k_gain, batch, kv_heads, n_rep, hd):
-    tokens, width = qkv.shape
-    seq = tokens // batch
+def attn_fwd(b, prev, qkv, cos_t, sin_t, q_gain, k_gain, batch, kv_heads, n_rep, hd):
+    seq, width = qkv.shape
     gw = width // kv_heads
     return pl.pallas_call(
-        functools.partial(attn_fwd_kernel, n_rep, hd, seq // 2),
-        grid=(batch, kv_heads),
-        in_specs=[pl.BlockSpec((seq, gw), lambda b, g: (b, g)),
-                  pl.BlockSpec((seq, hd), lambda b, g: (b, 0)),
-                  pl.BlockSpec((seq, hd), lambda b, g: (b, 0)),
-                  pl.BlockSpec((1, hd), lambda b, g: (0, 0)),
-                  pl.BlockSpec((1, hd), lambda b, g: (0, 0))],
-        out_specs=[pl.BlockSpec((seq, n_rep * hd), lambda b, g: (b, g))] + [pl.BlockSpec((seq, hd), lambda b, g: (b, g))] * n_rep,
-        out_shape=[jax.ShapeDtypeStruct((tokens, kv_heads * n_rep * hd), jnp.bfloat16)] + [jax.ShapeDtypeStruct((tokens, kv_heads * hd), jnp.bfloat16)] * n_rep,
-        cost_estimate=pl.CostEstimate(flops=25_000_000_000, bytes_accessed=14_000_000, transcendentals=8_400_000),
+        functools.partial(attn_fwd_kernel, n_rep, hd, seq // 2, len(prev)),
+        grid=(kv_heads,),
+        in_specs=[pl.BlockSpec((seq, gw), lambda g: (0, g)),
+                  pl.BlockSpec((seq, hd), lambda g: (b, 0)),
+                  pl.BlockSpec((seq, hd), lambda g: (b, 0)),
+                  pl.BlockSpec((1, hd), lambda g: (0, 0)),
+                  pl.BlockSpec((1, hd), lambda g: (0, 0))] + [pl.BlockSpec(memory_space=pl.ANY)] * len(prev),
+        out_specs=[pl.BlockSpec((seq, n_rep * hd), lambda g: (b, g))] + [pl.BlockSpec((seq, hd), lambda g: (b, g))] * n_rep,
+        out_shape=[jax.ShapeDtypeStruct((seq * batch, kv_heads * n_rep * hd), jnp.bfloat16)] + [jax.ShapeDtypeStruct((seq * batch, kv_heads * hd), jnp.bfloat16)] * n_rep,
+        input_output_aliases={5 + n: n for n in range(len(prev))},
+        cost_estimate=pl.CostEstimate(flops=12_000_000_000, bytes_accessed=8_000_000, transcendentals=4_200_000),
         name='attn_fwd',
-    )(qkv, cos_t, sin_t, q_gain, k_gain)
+    )(qkv, cos_t, sin_t, q_gain, k_gain, *prev)
 
 
 def attn_bwd_kernel(n_rep, hd, chunk, n_alias, qkv_ref, do_ref, cos_ref, sin_ref, qg_ref, kg_ref, *rest):
@@ -159,13 +160,13 @@
 
 
 def attn_bwd(b, prev, qkv, do, cos_t, sin_t, q_gain, k_gain, batch, kv_heads, n_rep, hd):
-    tokens, width = qkv.shape
-    seq = tokens // batch
+    seq, width = qkv.shape
+    tokens = seq * batch
     gw = width // kv_heads
     return pl.pallas_call(
         functools.partial(attn_bwd_kernel, n_rep, hd, seq // 2, len(prev)),
         grid=(kv_heads,),
-        in_specs=[pl.BlockSpec((seq, gw), lambda g: (b, g)),
+        in_specs=[pl.BlockSpec((seq, gw), lambda g: (0, g)),
                   pl.BlockSpec((seq, n_rep * hd), lambda g: (b, g)),
                   pl.BlockSpec((seq, hd), lambda g: (b, 0)),
                   pl.BlockSpec((seq, hd), lambda g: (b, 0)),
@@ -184,14 +185,17 @@
     )(qkv, do, cos_t, sin_t, q_gain, k_gain, *prev)
 
 
-def mlp_act_kernel(ff, n_chip, core_ref, gu_ref, act_ref, act_t_ref):
+def mlp_act_kernel(ff, n_chip, core_ref, gu_ref, act_ref, near_ref, far_ref):
     gate, up = gu_ref[:, :ff], gu_ref[:, ff:]
     act = gate * jax.nn.sigmoid(gate) * up
     act_ref[...] = act.astype(jnp.bfloat16)
     act_t = act.T.astype(jnp.bfloat16)
     block = ff // (2 * n_chip)
-    for i in range(2 * n_chip):
-        act_t_ref[lax.bitwise_xor(core_ref[0], i % 2), i // 2] = act_t[i * block:(i + 1) * block]
+    first = core_ref[0] == 0
+    for k in range(n_chip):
+        even, odd = act_t[2 * k * block:(2 * k + 1) * block], act_t[(2 * k + 1) * block:(2 * k + 2) * block]
+        near_ref[k * block:(k + 1) * block] = jnp.where(first, even, odd)
+        far_ref[k * block:(k + 1) * block] = jnp.where(first, odd, even)
 
 
 def mlp_act(gu, core, n_chip):
@@ -201,8 +205,8 @@
         functools.partial(mlp_act_kernel, ff, n_chip),
         grid=(tokens // rows,),
         in_specs=[pl.BlockSpec(memory_space=pltpu.SMEM), pl.BlockSpec((rows, 2 * ff), lambda i: (i, 0))],
-        out_specs=[pl.BlockSpec((rows, ff), lambda i: (i, 0)), pl.BlockSpec((2, n_chip, ff // (2 * n_chip), rows), lambda i: (0, 0, 0, i))],
-        out_shape=[jax.ShapeDtypeStruct((tokens, ff), jnp.bfloat16), jax.ShapeDtypeStruct((2, n_chip, ff // (2 * n_chip), tokens), jnp.bfloat16)],
+        out_specs=[pl.BlockSpec((rows, ff), lambda i: (i, 0)), pl.BlockSpec((ff // 2, rows), lambda i: (0, i)), pl.BlockSpec((ff // 2, rows), lambda i: (0, i))],
+        out_shape=[jax.ShapeDtypeStruct((tokens, ff), jnp.bfloat16), jax.ShapeDtypeStruct((ff // 2, tokens), jnp.bfloat16), jax.ShapeDtypeStruct((ff // 2, tokens), jnp.bfloat16)],
         cost_estimate=pl.CostEstimate(flops=12_000_000_000, bytes_accessed=38_000_000, transcendentals=3_200_000),
         name='mlp_act',
     )(core.reshape(1), gu)
@@ -227,6 +231,55 @@
         cost_estimate=pl.CostEstimate(flops=16_000_000_000, bytes_accessed=50_000_000, transcendentals=3_200_000),
         name='mlp_bwd',
     )(gu, grad_act)
+
+
+def pack_in_kernel(kv_heads, q_ref, k_ref, v_ref, gate_ref, up_ref, out_ref):
+    q_w, k_w = q_ref.shape[1] // kv_heads, k_ref.shape[1] // kv_heads
+    for g in range(kv_heads):
+        lo = g * (q_w + 2 * k_w)
+        out_ref[:, lo:lo + q_w] = q_ref[:, g * q_w:(g + 1) * q_w]
+        out_ref[:, lo + q_w:lo + q_w + k_w] = k_ref[:, g * k_w:(g + 1) * k_w]
+        out_ref[:, lo + q_w + k_w:lo + q_w + 2 * k_w] = v_ref[:, g * k_w:(g + 1) * k_w]
+    lo = kv_heads * (q_w + 2 * k_w)
+    out_ref[:, lo:lo + gate_ref.shape[1]] = gate_ref[...]
+    out_ref[:, lo + gate_ref.shape[1]:] = up_ref[...]
+
+
+def pack_in(kv_heads, *shards):
+    width = sum(w.shape[1] for w in shards)
+    return pl.pallas_call(
+        functools.partial(pack_in_kernel, kv_heads),
+        out_shape=jax.ShapeDtypeStruct((shards[0].shape[0], width), shards[0].dtype),
+        cost_estimate=pl.CostEstimate(flops=1_000_000, bytes_accessed=2_600_000, transcendentals=0),
+        name='pack_in',
+    )(*shards)
+
+
+def pack_tail_kernel(kv_heads, n_rep, hd, qkv_ref, out_rows_ref, out_ref):
+    rows, dim = qkv_ref.shape[0], out_ref.shape[1]
+    group, n_q = (n_rep + 2) * hd, kv_heads * n_rep * hd // dim
+    per = kv_heads // n_q
+    for g in range(kv_heads):
+        lo, p = g * group, (g // per) * rows
+        out_ref[p:p + rows, (g % per) * n_rep * hd:(g % per + 1) * n_rep * hd] = qkv_ref[:, lo:lo + n_rep * hd]
+        for j in range(2):
+            p = (n_q + j) * rows
+            out_ref[p:p + rows, g * hd:(g + 1) * hd] = qkv_ref[:, lo + (n_rep + j) * hd:lo + (n_rep + j + 1) * hd]
+    out_ref[(n_q + 2) * rows:] = out_rows_ref[...]
+
+
+def pack_tail(part_qkv, part_out, n_chip, kv_heads, n_rep, hd):
+    rows, out_rows, dim = part_qkv.shape[0] // n_chip, part_out.shape[0] // n_chip, part_out.shape[1]
+    block = part_qkv.shape[1] // dim * rows + out_rows
+    return pl.pallas_call(
+        functools.partial(pack_tail_kernel, kv_heads, n_rep, hd),
+        grid=(n_chip,),
+        in_specs=[pl.BlockSpec((rows, part_qkv.shape[1]), lambda i: (i, 0)), pl.BlockSpec((out_rows, dim), lambda i: (i, 0))],
+        out_specs=pl.BlockSpec((block, dim), lambda i: (i, 0)),
+        out_shape=jax.ShapeDtypeStruct((n_chip * block, dim), jnp.float32),
+        cost_estimate=pl.CostEstimate(flops=8_000_000_000, bytes_accessed=25_000_000, transcendentals=0),
+        name='pack_tail',
+    )(part_qkv, part_out)
 
 
 def solution(mesh):
@@ -269,13 +322,13 @@
         attn_gain = small[:, n_tok:n_tok + shard_rows].reshape(1, dim)
         mlp_gain = small[:, n_tok + shard_rows:].reshape(1, dim)
 
-        def group_columns(w):
-            return w.reshape(w.shape[0], kv_heads, -1)
-
-        qkv_shard = jnp.concatenate([group_columns(w_query), group_columns(w_key), group_columns(w_value)], axis=2).reshape(shard_rows, -1)
-        gu_shard = jnp.concatenate([w_gate, w_up], axis=1)
-        wqkv = gather(qkv_shard)
-        small, gu_shard, _ = lax.optimization_barrier((small, gu_shard, qkv_shard))
+        in_shard = pack_in(kv_heads, w_query, w_key, w_value, w_gate, w_up)
+        w_in = gather(in_shard)
+        qkv_cols = w_query.shape[1] + 2 * w_key.shape[1]
+        wqkv = w_in[:, :qkv_cols]
+        wgu = w_in[:, qkv_cols:]
+        wqkv, wgu = lax.optimization_barrier((wqkv, wgu))
+        small, _ = lax.optimization_barrier((small, in_shard))
         all_ids = small[:, :n_tok].astype(jnp.int32).reshape(n_chip, 2, batch, seq)
 
         def local_rows(ids, owner):
@@ -298,33 +351,40 @@
             merged = jnp.where(local_rows(near, me)[1], near_rows, jnp.where(local_rows(near, me + 1 - 2 * core)[1], recv, zero))
             return merged
 
-        wo = gather(w_out)
         merged = []
         for b in range(batch):
             merged.append(lookup(b))
             merged[b], all_ids = lax.optimization_barrier((merged[b], all_ids))
-        merged[-1], gu_shard, w_down = lax.optimization_barrier((merged[-1], gu_shard, w_down))
-        x_emb = jnp.concatenate([scatter_chips(m)[:seq] for m in merged], axis=0)
-        wgu = gather(gu_shard)
+        merged[-1], w_out, w_down = lax.optimization_barrier((merged[-1], w_out, w_down))
+        x_emb = [scatter_chips(m)[:seq] for m in merged]
+        wo = gather(w_out)
         wdown = gather(w_down)
 
         cos_t, sin_t = rope_tables(positions, hd)
         q_gain = q_norm.astype(jnp.float32)[None]
         k_gain = k_norm.astype(jnp.float32)[None]
 
-        normed1, norm1_inv = norm_fwd(x_emb)
-        attn_in = (normed1 * attn_gain).astype(jnp.bfloat16)
-        qkv = dot_nn(attn_in, wqkv).astype(jnp.bfloat16)
-        heads, *heads_rep = attn_fwd(qkv, cos_t, sin_t, q_gain, k_gain, batch, kv_heads, n_rep, hd)
-        hidden = (x_emb.astype(jnp.float32) + dot_nn(heads, wo)).astype(jnp.bfloat16)
+        normed1, norm1_inv, attn_in, qkv, heads = [], [], [], [], ()
+        for b in range(batch):
+            if b:
+                x_emb[b], heads = lax.optimization_barrier((x_emb[b], heads))
+            normed_b, inv_b = norm_fwd(x_emb[b])
+            normed1.append(normed_b)
+            norm1_inv.append(inv_b)
+            attn_in.append((normed_b * attn_gain).astype(jnp.bfloat16))
+            qkv.append(dot_nn(attn_in[b], wqkv).astype(jnp.bfloat16))
+            heads = attn_fwd(b, heads, qkv[b], cos_t, sin_t, q_gain, k_gain, batch, kv_heads, n_rep, hd)
+        heads, *heads_rep = heads
+        x_all = jnp.concatenate(x_emb, axis=0)
+        hidden = (x_all.astype(jnp.float32) + dot_nn(heads, wo)).astype(jnp.bfloat16)
         normed2, norm2_inv = norm_fwd(hidden)
         mlp_in = (normed2 * mlp_gain).astype(jnp.bfloat16)
         gu = dot_nn(mlp_in, wgu)
 
-        act, act_t = mlp_act(gu, core, n_chip)
+        act, near_act, far_act = mlp_act(gu, core, n_chip)
 
         dy = dy_out.reshape(n_tok, dim)
-        part_down = kdot_nn(act_t[0].reshape(-1, n_tok), dy) + swap_core(kdot_nn(act_t[1].reshape(-1, n_tok), dy))
+        part_down = kdot_nn(near_act, dy) + swap_core(kdot_nn(far_act, dy))
         dy_b, part_down = lax.optimization_barrier((dy, part_down))
         g_down = scatter_chips(part_down)
         grad_act = dot_nt(dy_b, wdown)
@@ -351,37 +411,36 @@
         hidden_b, part_gu = lax.optimization_barrier((hidden_b, part_gu))
         g_gu = scatter_chips(part_gu)
 
-        hidden_pad = jnp.pad(hidden_b, ((0, 0), (0, -dim % 384)))
         near_h = jnp.where(core == 0, heads_rep[0], heads_rep[1])
         far_h = jnp.where(core == 0, heads_rep[1], heads_rep[0])
-        recv_out = swap_core(dot_tn(far_h, hidden_pad))
+        recv_out = swap_core(dot_tn(far_h, hidden_b))
         grad_heads = dot_nt(hidden_b, wo).astype(jnp.bfloat16)
-        part_out = dot_tn(near_h, hidden_pad) + recv_out
-        g_out = scatter_chips(part_out)[:, :dim]
+        part_out = dot_tn(near_h, hidden_b) + recv_out
         local_ids = (all_ids - me * rows_local).reshape(n_dev, batch, seq)
         slots = jnp.where((local_ids >= 0) & (local_ids < rows_local), local_ids, rows_local)
         grad_attn_norm, grad_q_norm, grad_k_norm = 0.0, 0.0, 0.0
         dqkv, all_rows = (), []
         for b in range(batch):
             rows = slice(b * seq, (b + 1) * seq)
-            dqkv, dqg, dkg = attn_bwd(b, dqkv, qkv, grad_heads, cos_t, sin_t, q_gain, k_gain, batch, kv_heads, n_rep, hd)
+            dqkv, dqg, dkg = attn_bwd(b, dqkv, qkv[b], grad_heads, cos_t, sin_t, q_gain, k_gain, batch, kv_heads, n_rep, hd)
             grad_attn_in = dot_nt(dqkv[rows], wqkv)
-            grad_attn_norm += jnp.sum(grad_attn_in * normed1[rows], axis=0)
+            grad_attn_norm += jnp.sum(grad_attn_in * normed1[b], axis=0)
             grad_q_norm += jnp.sum(dqg, axis=0)
             grad_k_norm += jnp.sum(dkg, axis=0)
-            grad_x = grad_hidden[rows] + norm_bwd(grad_attn_in, normed1[rows], norm1_inv[rows], attn_gain)
+            grad_x = grad_hidden[rows] + norm_bwd(grad_attn_in, normed1[b], norm1_inv[b], attn_gain)
             grad_x, dqkv = lax.optimization_barrier((row_major(grad_x), dqkv))
             all_rows.append(gather(grad_x))
             dqkv = (dqkv,)
         dqkv, = dqkv
-        near1, far1 = split_cores(attn_in, -(-shard_rows // 24) * 24)
+        near1, far1 = split_cores(jnp.concatenate(attn_in, axis=0), shard_rows)
         far_qkv = dot_tn(far1, dqkv)
         part_qkv = dot_tn(near1, dqkv) + swap_core(far_qkv)
-        g_qkv = scatter_chips(part_qkv)[:shard_rows]
+        part_tail = pack_tail(part_qkv, part_out, n_chip, kv_heads, n_rep, hd)
+        g_tail = scatter_chips(part_tail)
         layer_out = (hidden.astype(jnp.float32) + dot_nn(act, wdown)).astype(jnp.bfloat16)
 
         vec = jnp.concatenate([grad_attn_norm, grad_mlp_norm, grad_q_norm, grad_k_norm])
-        vec, part_qkv, layer_out = lax.optimization_barrier((vec, part_qkv, layer_out))
+        vec, layer_out, _ = lax.optimization_barrier((vec, layer_out, part_tail))
         vec = jnp.sum(lax.all_gather(vec, AXIS_NAME), axis=0)
         g_attn_norm = lax.dynamic_slice_in_dim(vec[:dim], me * shard_rows, shard_rows)
         g_mlp_norm = lax.dynamic_slice_in_dim(vec[dim:2 * dim], me * shard_rows, shard_rows)
@@ -392,10 +451,11 @@
         for b in range(batch):
             d_table = d_table.at[slots[:, b].reshape(-1)].add(all_rows[b], mode='drop')
 
-        g_qkv = g_qkv.reshape(shard_rows, kv_heads, n_rep + 2, hd)
-        g_query = g_qkv[:, :, :n_rep].reshape(shard_rows, -1)
-        g_key = g_qkv[:, :, n_rep].reshape(shard_rows, -1)
-        g_value = g_qkv[:, :, n_rep + 1].reshape(shard_rows, -1)
+        n_q = w_query.shape[1] // dim
+        g_query = jnp.concatenate([g_tail[p * shard_rows:(p + 1) * shard_rows] for p in range(n_q)], axis=1)
+        g_key = g_tail[n_q * shard_rows:(n_q + 1) * shard_rows]
+        g_value = g_tail[(n_q + 1) * shard_rows:(n_q + 2) * shard_rows]
+        g_out = g_tail[(n_q + 2) * shard_rows:]
         return (layer_out.reshape(dy_out.shape), d_table, g_attn_norm, g_query, g_key, g_value, g_q_norm, g_k_norm, g_out, g_mlp_norm, g_gu[:, :ff], g_gu[:, ff:], g_down)
 
     return jax.shard_map(device_step, mesh=mesh, in_specs=(row_spec, row_spec, row_spec) + weight_specs + (batch_spec,), out_specs=(batch_spec, row_spec) + weight_specs, check_vma=False)

time: 1100 us -> 1150 us (1.045)
  waiting for transfers between devices: 339 us -> 378 us
  Pallas kernels: 136 us -> 151 us
    reduce_scatter x6 -> x5, waiting for transfers between devices: 307 us -> 357 us  [scatter_chips(): lax.psum_scatter(part, AXIS_NAME, scatter_dimension=0, tiled=True, axis_i...]
    pallas_call x1 -> x4, Pallas kernels: 34.7 us -> 50.3 us  [the longest x2 36.5 us: attn_fwd(): pl.pallas_call(functools.partial(attn_fwd_kernel, n_rep, hd, seq // 2, le...]
    slice x8 -> x7, local copies, waits for them, and re-layouts: 13.4 us -> 25 us  [the longest x1 11.5 us: device_step(): wgu = w_in[:, qkv_cols:]]
    dot_general x6 -> x7, matrix products: 69.8 us -> 67 us  [dot_nn(): lax.dot_general(split_rows(a), b, (((2,), (0,)), ((), ())), preferred_ele...]
  transfers between devices with their start and end apart: 18 -> 16, of which waited for: 6 -> 5; matrix products, arithmetic and copies ran while one was open for 43% -> 42% of each run, Pallas kernels for 11% -> 11%
where the time goes in v3:
time: 1150 us; the launch traced here: 1140 us
  waiting for transfers between devices  378 us (33%)
  other arithmetic  223 us (19%)
  matrix products  191 us (17%)
  local copies, waits for them, and re-layouts  151 us (13%)
  Pallas kernels  151 us (13%)
  blocking collectives  28.2 us (2%)
  between operations  16.4 us (1%)
    reduce_scatter x5, waiting for transfers between devices, scatter_chips(): lax.psum_scatter(part, AXIS_NAME, scatter_dimension=0, tiled=True, axis_i...  357 us
    scatter-add x2, other arithmetic, device_step(): d_table = d_table.at[slots[:, b].reshape(-1)].add(all_rows[b], mode='drop')  185 us
    gather x4, local copies, waits for them, and re-layouts, pick(): jnp.take(table_shard, jnp.clip(local, 0, rows_local - 1), axis=0, mode='c...  116 us
    pallas_call x2, Pallas kernels, attn_bwd(): pl.pallas_call(functools.partial(attn_bwd_kernel, n_rep, hd, seq // 2, le...  67.4 us
    dot_general x7, matrix products, dot_nn(): lax.dot_general(split_rows(a), b, (((2,), (0,)), ((), ())), preferred_ele...  67 us
    dot_general x5, matrix products, dot_nt(): lax.dot_general(split_rows(a), b, (((2,), (1,)), ((), ())), preferred_ele...  54.7 us
    dot_general x6, matrix products, dot_tn(): lax.dot_general(split_rows(a), split_rows(b), (((0, 1), (0, 1)), ((), ())...  54.4 us
    pallas_call x2, Pallas kernels, attn_fwd(): pl.pallas_call(functools.partial(attn_fwd_kernel, n_rep, hd, seq // 2, le...  36.5 us
  transfers between devices with their start and end apart: 16, of which 5 were waited for; matrix products, arithmetic and copies ran while one was open for 42% of the time, Pallas kernels for 11%

profile of v3, /device:TPU:0, one launch (start us, length us, event | category | flops | bytes accessed | tf_op | source)
XLA Modules:
  0.0 1140.8 jit_solution(232348231279547376)
XLA Ops:
  10.2 14.8 %all-gather.2 = f32[16,1,1152]{2,1,0:T(1,128)S(1)} all-gather(f32[1,1,1152]{2,1,0:T(1,128)S(1)} %reshape.444), channel_id=2, replica_groups=mesh['fsdp'=16] {'fsdp'}, dimensions={0}, use_global_device_ids=true | all-gather | bytes 78336 | tf_op jit(solution)/shard_map/all_gather | solution.py:321
  27.7 28.6 %gather_fusion.1 = bf16[4224,1024]{1,0:T(8,128)(2,1)} fusion(bf16[9504,1024]{1,0:T(8,128)(2,1)} %param.17, s32[5120]{0:T(1024)S(1)} %pad_clamp_fusion.2), kind=kCustom, calls=%fused_computation.1 | custom fusion | bytes 17318400 | tf_op jit(solution)/shard_map/jit(_take)/gather | solution.py:340
  57.0 28.6 %gather_fusion = bf16[4224,1024]{1,0:T(8,128)(2,1)} fusion(bf16[9504,1024]{1,0:T(8,128)(2,1)} %param.17, s32[5120]{0:T(1024)S(1)} %pad_clamp_fusion.3), kind=kCustom, calls=%fused_computation | custom fusion | bytes 17318400 | tf_op jit(solution)/shard_map/jit(_take)/gather | solution.py:340
  96.6 29.3 %gather_fusion.3 = bf16[4224,1024]{1,0:T(8,128)(2,1)} fusion(bf16[9504,1024]{1,0:T(8,128)(2,1)} %param.17, s32[5120]{0:T(1024)S(1)} %pad_clamp_fusion), kind=kCustom, calls=%fused_computation.3 | custom fusion | bytes 17318400 | tf_op jit(solution)/shard_map/jit(_take)/gather | solution.py:340
  126.4 29.1 %gather_fusion.2 = bf16[4224,1024]{1,0:T(8,128)(2,1)} fusion(bf16[9504,1024]{1,0:T(8,128)(2,1)} %param.17, s32[5120]{0:T(1024)S(1)} %pad_clamp_fusion.1), kind=kCustom, calls=%fused_computation.2 | custom fusion | bytes 17318400 | tf_op jit(solution)/shard_map/jit(_take)/gather | solution.py:340
  176.8 142.4 %reduce-scatter.8.cloned.1.call-done = bf16[528,1024]{1,0:T(8,128)(2,1)} async-done(((bf16[4224,1024]{1,0:T(8,128)(2,1)}), bf16[528,1024]{1,0:T(8,128)(2,1)}) %reduce-scatter.8.cloned.1.call-update) | async-done | bytes 1081360 | tf_op jit(solution)/shard_map/reduce_scatter | solution.py:300
  328.7 11.5 %slice.132 = bf16[1024,6144]{1,0:T(8,128)(2,1)} slice(bf16[1024,10240]{1,0:T(8,128)(2,1)} %all-gather.10.cloned.1.call-done), slice={[0:1024], [4096:10240]} | slice | bytes 25165824 | tf_op jit(solution)/shard_map/slice | solution.py:329
  346.4 18.3 %attn_fwd.2 = (bf16[1024,2048]{1,0:T(8,128)(2,1)}, bf16[1024,1024]{1,0:T(8,128)(2,1)}, bf16[1024,1024]{1,0:T(8,128)(2,1)}) custom-call(bf16[512,4096]{1,0:T(8,128)(2,1)} %convolution_convert_fusion.1.qkv_ref, f32[1024,128]{1,0:T(8,128)} %get-tuple-element.135.cos_ref, f32[1024,128]{1,0:T(8,128)} %get-tuple-element.136.sin_ref, ...), custom_call_target="tpu_custom_call" | custom-call | flops 12000000000 | bytes 8000000 | tf_op jit(solution)/shard_map/attn_fwd/pallas_call | solution.py:96
  375.9 18.2 %attn_fwd.3 = (bf16[1024,2048]{1,0:T(8,128)(2,1)}, bf16[1024,1024]{1,0:T(8,128)(2,1)}, bf16[1024,1024]{1,0:T(8,128)(2,1)}) custom-call(bf16[512,4096]{1,0:T(8,128)(2,1)} %convolution_convert_fusion.qkv_ref, f32[1024,128]{1,0:T(8,128)} %get-tuple-element.135.cos_ref, ...), custom_call_target="tpu_custom_call", output_to_operand_aliasing={{0}: (5, {}), {1}: (6, {}), {2}: (7, {})} | custom-call | flops 12000000000 | bytes 8000000 | tf_op jit(solution)/shard_map/attn_fwd/pallas_call | solution.py:96
  402.3 21.7 %fusion.66.gu_ref = f32[1024,6144]{1,0:T(8,128)} fusion(bf16[1024,6144]{1,0:T(8,128)(2,1)} %slice.132, bf16[1024,1024]{1,0:T(8,128)(2,1)S(1)} %get-tuple-element.131, f32[1024]{0:T(1024)S(1)} %mul.205, f32[1024]{0:T(1024)S(1)} %add_rsqrt_fusion), kind=kOutput, calls=%fused_computation.87 | convolution fusion | flops 12889096192 | bytes 39854080 | tf_op jit(solution)/shard_map/dot_general | solution.py:30
  424.0 15.1 %mlp_act.1 = (bf16[1024,3072]{1,0:T(8,128)(2,1)}, bf16[1536,1024]{1,0:T(8,128)(2,1)}, bf16[1536,1024]{1,0:T(8,128)(2,1)}) custom-call(s32[1]{0:T(128)} %bitcast.7.core_ref, f32[1024,6144]{1,0:T(8,128)} %fusion.66.gu_ref), custom_call_target="tpu_custom_call" | custom-call | flops 12000000000 | bytes 38000000 | tf_op jit(solution)/shard_map/mlp_act/pallas_call | solution.py:204
  464.1 12.7 %fusion.84.ga_ref = f32[1024,3072]{1,0:T(8,128)} fusion(bf16[1024,1024]{1,0:T(8,128)(2,1)S(1)} %bitcast.78, bf16[3072,1024]{1,0:T(8,128)(2,1)} %all-gather.14.cloned.1.call-done), kind=kOutput, calls=%fused_computation.143 | convolution fusion | flops 6442450944 | bytes 20971520 | tf_op jit(solution)/shard_map/dot_general | solution.py:34
  476.8 18.2 %mlp_bwd.1 = bf16[1024,6144]{1,0:T(8,128)(2,1)} custom-call(f32[1024,6144]{1,0:T(8,128)} %fusion.66.gu_ref, f32[1024,3072]{1,0:T(8,128)} %fusion.84.ga_ref), custom_call_target="tpu_custom_call" | custom-call | flops 16000000000 | bytes 50000000 | tf_op jit(solution)/shard_map/mlp_bwd/pallas_call | solution.py:225
  495.0 12.9 %fusion.64 = f32[512,6144]{1,0:T(8,128)} fusion(bf16[1024,6144]{1,0:T(8,128)(2,1)} %mlp_bwd.1, bf16[1024,1024]{1,0:T(8,128)(2,1)} %fusion.56), kind=kOutput, calls=%fused_computation.83 | convolution fusion | flops 6442450944 | bytes 26214400 | tf_op jit(solution)/shard_map/dot_general | solution.py:38
  508.0 17.7 %fusion.11 = (f32[1024]{0:T(1024)}, f32[1024]{0:T(1024)S(1)}, f32[1024,1024]{1,0:T(8,128)S(1)}) fusion(bf16[1024,1024]{1,0:T(8,128)(2,1)S(1)} %copy-done.10, f32[1024]{0:T(1024)S(1)} %add_rsqrt_fusion, f32[1024]{0:T(1024)S(1)} %mul.205, bf16[1024,6144]{1,0:T(8,128)(2,1)S(1)} %copy-done, bf16[1024,6144]{1,0:T(8,128)(2,1)} %slice.132), kind=kOutput, calls=%fused_computation.27 | convolution fusion | flops 12892239872 | bytes 31473664 | tf_op jit(solution)/shard_map/dot_general | solution.py:34
  529.2 12.9 %convolution_add_fusion = f32[512,6144]{1,0:T(8,128)} fusion(f32[512,6144]{1,0:T(8,128)} %collective-permute-done.3, bf16[1024,6144]{1,0:T(8,128)(2,1)S(1)} %copy-done, bf16[1024,1024]{1,0:T(8,128)(2,1)} %fusion.56), kind=kOutput, calls=%fused_computation.8 | convolution fusion | flops 6445596672 | bytes 38797312 | tf_op jit(solution)/shard_map/dot_general | solution.py:38
  553.5 33.9 %attn_bwd.2 = (bf16[1024,4096]{1,0:T(8,128)(2,1)}, f32[8,128]{1,0:T(8,128)}, f32[8,128]{1,0:T(8,128)}) custom-call(bf16[512,4096]{1,0:T(8,128)(2,1)} %convolution_convert_fusion.1.qkv_ref, bf16[1024,2048]{1,0:T(8,128)(2,1)} %convolution_convert_fusion.2.do_ref, f32[1024,128]{1,0:T(8,128)} %get-tuple-element.135.cos_ref, ...), custom_call_target="tpu_custom_call" | custom-call | flops 24999999488 | bytes 14000000 | tf_op jit(solution)/shard_map/attn_bwd/pallas_call | solution.py:166
  598.1 33.5 %attn_bwd.3 = (bf16[1024,4096]{1,0:T(8,128)(2,1)}, f32[8,128]{1,0:T(8,128)}, f32[8,128]{1,0:T(8,128)}) custom-call(bf16[512,4096]{1,0:T(8,128)(2,1)} %convolution_convert_fusion.qkv_ref, bf16[1024,2048]{1,0:T(8,128)(2,1)} %convolution_convert_fusion.2.do_ref, f32[1024,128]{1,0:T(8,128)} %get-tuple-element.135.cos_ref, ...), custom_call_target="tpu_custom_call", output_to_operand_aliasing={{0}: (6, {})} | custom-call | flops 24999999488 | bytes 14000000 | tf_op jit(solution)/shard_map/attn_bwd/pallas_call | solution.py:166
  658.5 13.9 %collective-permute-done.5 = f32[1024,1024]{1,0:T(8,128)S(1)} collective-permute-done((f32[1024,1024]{1,0:T(8,128)S(1)}, f32[1024,1024]{1,0:T(8,128)S(1)}, u32[]{:S(2)}, u32[]{:S(2)}) %collective-permute-start.5) | collective-permute-done | bytes 4194336 | tf_op jit(solution)/shard_map/ppermute | solution.py:303
  699.7 12.3 %fusion.13 = bf16[1024,1024]{1,0:T(8,128)(2,1)} fusion(bf16[1024,1024]{1,0:T(8,128)(2,1)S(1)} %copy-done.11, bf16[1024,3072]{1,0:T(8,128)(2,1)} %get-tuple-element.84, bf16[3072,1024]{1,0:T(8,128)(2,1)} %all-gather.14.cloned.1.call-done), kind=kOutput, calls=%fused_computation.29 | convolution fusion | flops 6445596672 | bytes 16777216 | tf_op jit(solution)/shard_map/dot_general | solution.py:30
  712.2 13.5 %all-gather.3 = f32[16,1,2304]{2,1,0:T(1,128)S(1)} all-gather(f32[1,1,2304]{2,1,0:T(1,128)S(1)} %reshape.446), channel_id=3, replica_groups=mesh['fsdp'=16] {'fsdp'}, dimensions={0}, use_global_device_ids=true | all-gather | bytes 156672 | tf_op jit(solution)/shard_map/all_gather | solution.py:444
  730.1 213.1 %reduce-scatter.10.cloned.1.call-done = f32[384,1024]{1,0:T(8,128)} async-done(((f32[3072,1024]{1,0:T(8,128)}), f32[384,1024]{1,0:T(8,128)}) %reduce-scatter.10.cloned.1.call-update) | async-done | bytes 1572880 | tf_op jit(solution)/shard_map/reduce_scatter | solution.py:300
  948.0 87.8 %scatter_custom_fusion = f32[9504,1024]{1,0:T(8,128)} fusion(s32[8192]{0:T(1024)S(1)} %bitcast.86, f32[8192,1024]{1,0:T(8,128)} %all-gather.16.cloned.1.call-done, f32[]{:T(128)} %constant.65.clone.1), kind=kCustom, calls=%fused_computation.6 | custom fusion | flops 8388608 | bytes 38928896 | tf_op jit(solution)/shard_map/scatter-add | solution.py:452
  1035.9 97.4 %scatter_fusion = f32[9504,1024]{1,0:T(8,128)} fusion(f32[9504,1024]{1,0:T(8,128)} %scatter_custom_fusion, s32[8192]{0:T(1024)S(1)} %bitcast.83, f32[8192,1024]{1,0:T(8,128)} %all-gather.18.cloned.1.call-done), kind=kCustom, calls=%fused_computation.5 | custom fusion | flops 8388608 | bytes 100696064 | tf_op jit(solution)/shard_map/scatter-add | solution.py:452
  (217 shorter events, 187.2 us)
Async XLA Ops:
  8.0 165.0 %reduce-scatter.6.cloned.1.call-start = ((), (), s32[]{:S(2)}) async-start(), calls=%async_computation.5 | async-start | bytes 9732096 | tf_op jit(solution)/shard_map/reduce_scatter | solution.py:300
  27.5 68.9 %copy-start.17 = (s32[8,2,2,512]{3,2,1,0:T(2,128)}, s32[8,2,2,512]{3,2,1,0:T(2,128)S(1)}, u32[]{:S(2)}) copy-start(s32[8,2,2,512]{3,2,1,0:T(2,128)S(1)} %reshape.375) | copy-start | bytes 196612
  56.3 29.3 %collective-permute-start = (bf16[4224,1024]{1,0:T(8,128)(2,1)}, bf16[4224,1024]{1,0:T(8,128)(2,1)}, u32[]{:S(2)}, u32[]{:S(2)}) collective-permute-start(bf16[4224,1024]{1,0:T(8,128)(2,1)} %gather_fusion.1), channel_id=1, source_target_pairs={{0,1},{1,0},{2,3},{3,2},{4,5},{5,4},{6,7},{7,6},{8,9},{9,8},{10,11... | collective-permute-start | bytes 25952264 | tf_op jit(solution)/shard_map/ppermute | solution.py:303
  95.9 223.3 %reduce-scatter.8.cloned.1.call-start = ((), (), s32[]{:S(2)}) async-start(), calls=%async_computation.7 | async-start | bytes 9732096 | tf_op jit(solution)/shard_map/reduce_scatter | solution.py:300
  125.9 29.5 %collective-permute-start.1 = (bf16[4224,1024]{1,0:T(8,128)(2,1)}, bf16[4224,1024]{1,0:T(8,128)(2,1)}, u32[]{:S(2)}, u32[]{:S(2)}) collective-permute-start(bf16[4224,1024]{1,0:T(8,128)(2,1)} %gather_fusion.3), channel_id=1, source_target_pairs={{0,1},{1,0},{2,3},{3,2},{4,5},{5,4},{6,7},{7,6},{8,9},{9,8},{10,11... | collective-permute-start | bytes 25952264 | tf_op jit(solution)/shard_map/ppermute | solution.py:303
  166.4 154.2 %all-gather.10.cloned.1.call-start = ((), (), s32[]{:S(2)}) async-start(), calls=%async_computation.6 | async-start | bytes 22282240 | tf_op jit(solution)/shard_map/all_gather | solution.py:297
  167.0 227.2 %all-gather.12.cloned.1.call-start = ((), (), s32[]{:S(2)}) async-start(), calls=%async_computation.8 | async-start | bytes 4456448 | tf_op jit(solution)/shard_map/all_gather | solution.py:297
  167.6 296.5 %all-gather.14.cloned.1.call-start = ((), (), s32[]{:S(2)}) async-start(), calls=%async_computation.9 | async-start | bytes 6684672 | tf_op jit(solution)/shard_map/all_gather | solution.py:297
  167.9 197.1 %copy-start.19 = (f32[1024]{0:T(1024)}, f32[1024]{0:T(1024)S(1)}, u32[]{:S(2)}) copy-start(f32[1024]{0:T(1024)S(1)} %mul.189) | copy-start | bytes 12292
  171.7 555.8 %reduce-scatter.12.cloned.1.call-start = ((), (), s32[]{:S(2)}) async-start(), calls=%async_computation.13 | async-start | bytes 14155776 | tf_op jit(solution)/shard_map/reduce_scatter | solution.py:300
  176.8 163.5 %copy-start.14 = (bf16[512,1024]{1,0:T(8,128)(2,1)}, bf16[512,1024]{1,0:T(8,128)(2,1)S(1)}, u32[]{:S(2)}) copy-start(bf16[512,1024]{1,0:T(8,128)(2,1)S(1)} %fusion.28) | copy-start | bytes 3145732
  320.5 73.6 %copy-start.1 = (bf16[512,1024]{1,0:T(8,128)(2,1)}, bf16[512,1024]{1,0:T(8,128)(2,1)S(1)}, u32[]{:S(2)}) copy-start(bf16[512,1024]{1,0:T(8,128)(2,1)S(1)} %slice.134) | copy-start | bytes 3145732
  446.4 10.5 collective-permute-start.2
  507.8 21.4 %collective-permute-start.3 = (f32[512,6144]{1,0:T(8,128)}, f32[512,6144]{1,0:T(8,128)}, u32[]{:S(2)}, u32[]{:S(2)}) collective-permute-start(f32[512,6144]{1,0:T(8,128)} %fusion.64), channel_id=1, source_target_pairs={{0,1},{1,0},{2,3},{3,2},{4,5},{5,4},{6,7},{7,6},{8,9},{9,8},{10,11... | collective-permute-start | bytes 37748744 | tf_op jit(solution)/shard_map/ppermute | solution.py:303
  542.1 401.1 %reduce-scatter.10.cloned.1.call-start = ((), (), s32[]{:S(2)}) async-start(), calls=%async_computation.12 | async-start | bytes 14155776 | tf_op jit(solution)/shard_map/reduce_scatter | solution.py:300
  553.5 33.9 %copy-start.5 = (bf16[528,1024]{1,0:T(8,128)(2,1)S(1)}, bf16[528,1024]{1,0:T(8,128)(2,1)}, u32[]{:S(2)}) copy-start(bf16[528,1024]{1,0:T(8,128)(2,1)} %reduce-scatter.6.cloned.1.call-done) | copy-start | bytes 3244036
  553.5 33.9 %copy-start.20 = (f32[1024]{0:T(1024)S(1)}, f32[1024]{0:T(1024)}, u32[]{:S(2)}) copy-start(f32[1024]{0:T(1024)} %copy-done.19) | copy-start | bytes 12292
  553.5 33.9 %copy-start.22 = (f32[512]{0:T(512)S(1)}, f32[512]{0:T(512)}, u32[]{:S(2)}) copy-start(f32[512]{0:T(512)} %copy-done.21) | copy-start | bytes 6148
  598.1 33.5 %copy-start.24 = (f32[512]{0:T(512)S(1)}, f32[512]{0:T(512)}, u32[]{:S(2)}) copy-start(f32[512]{0:T(512)} %copy-done.23) | copy-start | bytes 6148
  653.0 23.8 %collective-permute-start.4 = (f32[512,4096]{1,0:T(8,128)}, f32[512,4096]{1,0:T(8,128)}, u32[]{:S(2)}, u32[]{:S(2)}) collective-permute-start(f32[512,4096]{1,0:T(8,128)} %fusion.60), channel_id=1, source_target_pairs={{0,1},{1,0},{2,3},{3,2},{4,5},{5,4},{6,7},{7,6},{8,9},{9,8},{10,11... | collective-permute-start | bytes 25165832 | tf_op jit(solution)/shard_map/ppermute | solution.py:303
  658.0 14.4 %collective-permute-start.5 = (f32[1024,1024]{1,0:T(8,128)S(1)}, f32[1024,1024]{1,0:T(8,128)S(1)}, u32[]{:S(2)}, u32[]{:S(2)}) collective-permute-start(f32[1024,1024]{1,0:T(8,128)S(1)} %fusion.45), channel_id=1, source_target_pairs={{0,1},{1,0},{2,3},{3,2},{4,5},{5,4},{6,7},{7,6},{8,9},{9,8},{10,11... | collective-permute-start | bytes 12582920 | tf_op jit(solution)/shard_map/ppermute | solution.py:303
  697.3 250.7 %all-gather.16.cloned.1.call-start = ((), (), s32[]{:S(2)}) async-start(), calls=%async_computation.10 | async-start | bytes 35651584 | tf_op jit(solution)/shard_map/all_gather | solution.py:297
  698.1 337.8 %all-gather.18.cloned.1.call-start = ((), (), s32[]{:S(2)}) async-start(), calls=%async_computation.11 | async-start | bytes 35651584 | tf_op jit(solution)/shard_map/all_gather | solution.py:297
  698.8 434.5 %reduce-scatter.14.cloned.1.call-start = ((), (), s32[]{:S(2)}) async-start(), calls=%async_computation.14 | async-start | bytes 7077888 | tf_op jit(solution)/shard_map/reduce_scatter | solution.py:300
  (32 other events, 359.5 us)
Sparse Core Ops, SparseCore 0:
  96.0 76.9 reduce-scatter.5
  177.8 141.2 reduce-scatter.7
  542.3 102.3 reduce-scatter.11
  697.4 245.7 reduce-scatter.9
  947.6 108.2 reduce-scatter.13
Sparse Core Ops, SparseCore 1:
  169.7 98.6 all-gather.9
  270.5 41.4 all-gather.11
  314.1 42.0 all-gather.13
  700.3 155.2 all-gather.15
  857.9 147.3 all-gather.17

commit v4 on v3

--- a/solution.py
+++ b/solution.py
@@ -185,55 +185,74 @@
     )(qkv, do, cos_t, sin_t, q_gain, k_gain, *prev)
 
 
-def mlp_act_kernel(ff, n_chip, core_ref, gu_ref, act_ref, near_ref, far_ref):
-    gate, up = gu_ref[:, :ff], gu_ref[:, ff:]
-    act = gate * jax.nn.sigmoid(gate) * up
-    act_ref[...] = act.astype(jnp.bfloat16)
-    act_t = act.T.astype(jnp.bfloat16)
-    block = ff // (2 * n_chip)
+def mlp_fwd_kernel(core_ref, x_ref, w_ref, gu_ref, act_ref, near_ref, far_ref):
+    tile, block, chunk = act_ref.shape[1], near_ref.shape[0], 256
     first = core_ref[0] == 0
-    for k in range(n_chip):
-        even, odd = act_t[2 * k * block:(2 * k + 1) * block], act_t[(2 * k + 1) * block:(2 * k + 2) * block]
-        near_ref[k * block:(k + 1) * block] = jnp.where(first, even, odd)
-        far_ref[k * block:(k + 1) * block] = jnp.where(first, odd, even)
-
-
-def mlp_act(gu, core, n_chip):
-    tokens, ff = gu.shape[0], gu.shape[1] // 2
-    rows = 128
-    return pl.pallas_call(
-        functools.partial(mlp_act_kernel, ff, n_chip),
-        grid=(tokens // rows,),
-        in_specs=[pl.BlockSpec(memory_space=pltpu.SMEM), pl.BlockSpec((rows, 2 * ff), lambda i: (i, 0))],
-        out_specs=[pl.BlockSpec((rows, ff), lambda i: (i, 0)), pl.BlockSpec((ff // 2, rows), lambda i: (0, i)), pl.BlockSpec((ff // 2, rows), lambda i: (0, i))],
-        out_shape=[jax.ShapeDtypeStruct((tokens, ff), jnp.bfloat16), jax.ShapeDtypeStruct((ff // 2, tokens), jnp.bfloat16), jax.ShapeDtypeStruct((ff // 2, tokens), jnp.bfloat16)],
-        cost_estimate=pl.CostEstimate(flops=12_000_000_000, bytes_accessed=38_000_000, transcendentals=3_200_000),
-        name='mlp_act',
-    )(core.reshape(1), gu)
-
-
-def mlp_bwd_kernel(ff, gu_ref, ga_ref, out_ref):
-    gate, up, grad_act = gu_ref[:, :ff], gu_ref[:, ff:], ga_ref[...]
-    sig = jax.nn.sigmoid(gate)
-    out_ref[:, :ff] = (grad_act * up * sig * (1.0 + gate * (1.0 - sig))).astype(jnp.bfloat16)
-    out_ref[:, ff:] = (grad_act * gate * sig).astype(jnp.bfloat16)
-
-
-def mlp_bwd(gu, grad_act):
-    tokens, ff = grad_act.shape
-    rows = 128
-    return pl.pallas_call(
-        functools.partial(mlp_bwd_kernel, ff),
-        grid=(tokens // rows,),
-        in_specs=[pl.BlockSpec((rows, 2 * ff), lambda i: (i, 0)), pl.BlockSpec((rows, ff), lambda i: (i, 0))],
-        out_specs=pl.BlockSpec((rows, 2 * ff), lambda i: (i, 0)),
-        out_shape=jax.ShapeDtypeStruct((tokens, 2 * ff), jnp.bfloat16),
-        cost_estimate=pl.CostEstimate(flops=16_000_000_000, bytes_accessed=50_000_000, transcendentals=3_200_000),
+    for lo in range(0, x_ref.shape[0], chunk):
+        gu = kdot_nn(x_ref[lo:lo + chunk], w_ref[...])
+        gu_ref[lo:lo + chunk] = gu
+        gate = gu[:, :tile]
+        act = gate * jax.nn.sigmoid(gate) * gu[:, tile:]
+        act_ref[lo:lo + chunk] = act.astype(jnp.bfloat16)
+        act_t = act.T.astype(jnp.bfloat16)
+        near_ref[:, lo:lo + chunk] = jnp.where(first, act_t[:block], act_t[block:])
+        far_ref[:, lo:lo + chunk] = jnp.where(first, act_t[block:], act_t[:block])
+
+
+def mlp_fwd(x, wgu, core, n_chip):
+    tokens, dim = x.shape
+    ff = wgu.shape[1] // 2
+    tile = ff // n_chip
+    half = pl.BlockSpec((tile // 2, tokens), lambda i: (i, 0))
+    return pl.pallas_call(
+        mlp_fwd_kernel,
+        grid=(n_chip,),
+        in_specs=[pl.BlockSpec(memory_space=pltpu.SMEM), pl.BlockSpec((tokens, dim), lambda i: (0, 0)), pl.BlockSpec((dim, 2 * tile), lambda i: (0, i))],
+        out_specs=[pl.BlockSpec((tokens, 2 * tile), lambda i: (0, i)), pl.BlockSpec((tokens, tile), lambda i: (0, i)), half, half],
+        out_shape=[jax.ShapeDtypeStruct((tokens, 2 * ff), jnp.float32), jax.ShapeDtypeStruct((tokens, ff), jnp.bfloat16),
+                   jax.ShapeDtypeStruct((ff // 2, tokens), jnp.bfloat16), jax.ShapeDtypeStruct((ff // 2, tokens), jnp.bfloat16)],
+        cost_estimate=pl.CostEstimate(flops=16_000_000_000, bytes_accessed=52_000_000, transcendentals=3_200_000),
+        name='mlp_fwd',
+    )(core.reshape(1), x, wgu)
+
+
+def mlp_bwd_kernel(dy_ref, w_ref, gu_ref, out_ref):
+    tile, chunk = w_ref.shape[0], 256
+    for lo in range(0, dy_ref.shape[0], chunk):
+        grad_act = kdot_nt(dy_ref[lo:lo + chunk], w_ref[...])
+        gate, up = gu_ref[lo:lo + chunk, :tile], gu_ref[lo:lo + chunk, tile:]
+        sig = jax.nn.sigmoid(gate)
+        out_ref[lo:lo + chunk, :tile] = (grad_act * up * sig * (1.0 + gate * (1.0 - sig))).astype(jnp.bfloat16)
+        out_ref[lo:lo + chunk, tile:] = (grad_act * gate * sig).astype(jnp.bfloat16)
+
+
+def mlp_bwd(dy, wdown, gu, n_chip):
+    tokens, dim = dy.shape
+    tile = wdown.shape[0] // n_chip
+    return pl.pallas_call(
+        mlp_bwd_kernel,
+        grid=(n_chip,),
+        in_specs=[pl.BlockSpec((tokens, dim), lambda i: (0, 0)), pl.BlockSpec((tile, dim), lambda i: (i, 0)), pl.BlockSpec((tokens, 2 * tile), lambda i: (0, i))],
+        out_specs=pl.BlockSpec((tokens, 2 * tile), lambda i: (0, i)),
+        out_shape=jax.ShapeDtypeStruct(gu.shape, jnp.bfloat16),
+        cost_estimate=pl.CostEstimate(flops=12_000_000_000, bytes_accessed=46_000_000, transcendentals=3_200_000),
         name='mlp_bwd',
-    )(gu, grad_act)
-
-
-def pack_in_kernel(kv_heads, q_ref, k_ref, v_ref, gate_ref, up_ref, out_ref):
+    )(dy, wdown, gu)
+
+
+def unpack_gu_kernel(n_tiles, in_ref, gate_ref, up_ref):
+    tile = gate_ref.shape[1] // n_tiles
+    for i in range(n_tiles):
+        gate_ref[:, i * tile:(i + 1) * tile] = in_ref[:, 2 * i * tile:(2 * i + 1) * tile]
+        up_ref[:, i * tile:(i + 1) * tile] = in_ref[:, (2 * i + 1) * tile:(2 * i + 2) * tile]
+
+
+def unpack_gu(g_gu, n_tiles):
+    shape = jax.ShapeDtypeStruct((g_gu.shape[0], g_gu.shape[1] // 2), g_gu.dtype)
+    return pl.pallas_call(functools.partial(unpack_gu_kernel, n_tiles), out_shape=[shape, shape], name='unpack_gu')(g_gu)
+
+
+def pack_in_kernel(kv_heads, n_tiles, q_ref, k_ref, v_ref, gate_ref, up_ref, out_ref):
     q_w, k_w = q_ref.shape[1] // kv_heads, k_ref.shape[1] // kv_heads
     for g in range(kv_heads):
         lo = g * (q_w + 2 * k_w)
@@ -241,14 +260,16 @@
         out_ref[:, lo + q_w:lo + q_w + k_w] = k_ref[:, g * k_w:(g + 1) * k_w]
         out_ref[:, lo + q_w + k_w:lo + q_w + 2 * k_w] = v_ref[:, g * k_w:(g + 1) * k_w]
     lo = kv_heads * (q_w + 2 * k_w)
-    out_ref[:, lo:lo + gate_ref.shape[1]] = gate_ref[...]
-    out_ref[:, lo + gate_ref.shape[1]:] = up_ref[...]
-
-
-def pack_in(kv_heads, *shards):
+    tile = gate_ref.shape[1] // n_tiles
+    for i in range(n_tiles):
+        out_ref[:, lo + 2 * i * tile:lo + (2 * i + 1) * tile] = gate_ref[:, i * tile:(i + 1) * tile]
+        out_ref[:, lo + (2 * i + 1) * tile:lo + (2 * i + 2) * tile] = up_ref[:, i * tile:(i + 1) * tile]
+
+
+def pack_in(kv_heads, n_tiles, *shards):
     width = sum(w.shape[1] for w in shards)
     return pl.pallas_call(
-        functools.partial(pack_in_kernel, kv_heads),
+        functools.partial(pack_in_kernel, kv_heads, n_tiles),
         out_shape=jax.ShapeDtypeStruct((shards[0].shape[0], width), shards[0].dtype),
         cost_estimate=pl.CostEstimate(flops=1_000_000, bytes_accessed=2_600_000, transcendentals=0),
         name='pack_in',
@@ -311,7 +332,6 @@
         hd = q_norm.shape[0]
         kv_heads = w_key.shape[1] // hd
         n_rep = w_query.shape[1] // w_key.shape[1]
-        ff = w_gate.shape[1]
         shard_rows = w_query.shape[0]
 
         def near_far(blocks, axis):
@@ -322,7 +342,7 @@
         attn_gain = small[:, n_tok:n_tok + shard_rows].reshape(1, dim)
         mlp_gain = small[:, n_tok + shard_rows:].reshape(1, dim)
 
-        in_shard = pack_in(kv_heads, w_query, w_key, w_value, w_gate, w_up)
+        in_shard = pack_in(kv_heads, n_chip, w_query, w_key, w_value, w_gate, w_up)
         w_in = gather(in_shard)
         qkv_cols = w_query.shape[1] + 2 * w_key.shape[1]
         wqkv = w_in[:, :qkv_cols]
@@ -379,16 +399,14 @@
         hidden = (x_all.astype(jnp.float32) + dot_nn(heads, wo)).astype(jnp.bfloat16)
         normed2, norm2_inv = norm_fwd(hidden)
         mlp_in = (normed2 * mlp_gain).astype(jnp.bfloat16)
-        gu = dot_nn(mlp_in, wgu)
-
-        act, near_act, far_act = mlp_act(gu, core, n_chip)
+        gu, act, near_act, far_act = mlp_fwd(mlp_in, wgu, core, n_chip)
+
 
         dy = dy_out.reshape(n_tok, dim)
         part_down = kdot_nn(near_act, dy) + swap_core(kdot_nn(far_act, dy))
         dy_b, part_down = lax.optimization_barrier((dy, part_down))
         g_down = scatter_chips(part_down)
-        grad_act = dot_nt(dy_b, wdown)
-        dgu = mlp_bwd(gu, grad_act)
+        dgu = mlp_bwd(dy_b, wdown, gu, n_chip)
 
         row_ids = jnp.arange(dim)
 
@@ -456,6 +474,7 @@
         g_key = g_tail[n_q * shard_rows:(n_q + 1) * shard_rows]
         g_value = g_tail[(n_q + 1) * shard_rows:(n_q + 2) * shard_rows]
         g_out = g_tail[(n_q + 2) * shard_rows:]
-        return (layer_out.reshape(dy_out.shape), d_table, g_attn_norm, g_query, g_key, g_value, g_q_norm, g_k_norm, g_out, g_mlp_norm, g_gu[:, :ff], g_gu[:, ff:], g_down)
+        g_gate, g_up = unpack_gu(g_gu, n_chip)
+        return (layer_out.reshape(dy_out.shape), d_table, g_attn_norm, g_query, g_key, g_value, g_q_norm, g_k_norm, g_out, g_mlp_norm, g_gate, g_up, g_down)
 
     return jax.shard_map(device_step, mesh=mesh, in_specs=(row_spec, row_spec, row_spec) + weight_specs + (batch_spec,), out_specs=(batch_spec, row_spec) + weight_specs, check_vma=False)

time: 1150 us -> 1130 us (0.983)
  matrix products: 191 us -> 156 us
  Pallas kernels: 151 us -> 164 us
    dot_general x7 -> x6, matrix products: 67 us -> 45.3 us  [dot_nn(): lax.dot_general(split_rows(a), b, (((2,), (0,)), ((), ())), preferred_ele...]
    pallas_call x3 -> x4, Pallas kernels: 35.7 us -> 48.7 us  [the longest x1 22 us: mlp_fwd(): pl.pallas_call(mlp_fwd_kernel, grid=(n_chip,), in_specs=[pl.BlockSpec(mem...]
    dot_general x5 -> x4, matrix products: 54.7 us -> 41.9 us  [dot_nt(): lax.dot_general(split_rows(a), b, (((2,), (1,)), ((), ())), preferred_ele...]
  transfers between devices with their start and end apart: 16 -> 16, of which waited for: 5 -> 5; matrix products, arithmetic and copies ran while one was open for 42% -> 41% of each run, Pallas kernels for 11% -> 12%
where the time goes in v4:
time: 1130 us; the launch traced here: 1120 us
  waiting for transfers between devices  378 us (33%)
  other arithmetic  226 us (20%)
  Pallas kernels  164 us (15%)
  matrix products  156 us (14%)
  local copies, waits for them, and re-layouts  148 us (13%)
  blocking collectives  28.1 us (2%)
  between operations  16.7 us (1%)
    reduce_scatter x5, waiting for transfers between devices, scatter_chips(): lax.psum_scatter(part, AXIS_NAME, scatter_dimension=0, tiled=True, axis_i...  357 us
    scatter-add x2, other arithmetic, device_step(): d_table = d_table.at[slots[:, b].reshape(-1)].add(all_rows[b], mode='drop')  185 us
    gather x4, local copies, waits for them, and re-layouts, pick(): jnp.take(table_shard, jnp.clip(local, 0, rows_local - 1), axis=0, mode='c...  116 us
    pallas_call x2, Pallas kernels, attn_bwd(): pl.pallas_call(functools.partial(attn_bwd_kernel, n_rep, hd, seq // 2, le...  67.4 us
    dot_general x6, matrix products, dot_tn(): lax.dot_general(split_rows(a), split_rows(b), (((0, 1), (0, 1)), ((), ())...  54.4 us
    dot_general x6, matrix products, dot_nn(): lax.dot_general(split_rows(a), b, (((2,), (0,)), ((), ())), preferred_ele...  45.3 us
    dot_general x4, matrix products, dot_nt(): lax.dot_general(split_rows(a), b, (((2,), (1,)), ((), ())), preferred_ele...  41.9 us
    pallas_call x2, Pallas kernels, attn_fwd(): pl.pallas_call(functools.partial(attn_fwd_kernel, n_rep, hd, seq // 2, le...  36.4 us
  transfers between devices with their start and end apart: 16, of which 5 were waited for; matrix products, arithmetic and copies ran while one was open for 41% of the time, Pallas kernels for 12%

profile of v4, /device:TPU:0, one launch (start us, length us, event | category | flops | bytes accessed | tf_op | source)
XLA Modules:
  0.0 1118.8 jit_solution(3909352830444647636)
XLA Ops:
  10.2 14.8 %all-gather.2 = f32[16,1,1152]{2,1,0:T(1,128)S(1)} all-gather(f32[1,1,1152]{2,1,0:T(1,128)S(1)} %reshape.436), channel_id=2, replica_groups=mesh['fsdp'=16] {'fsdp'}, dimensions={0}, use_global_device_ids=true | all-gather | bytes 78336 | tf_op jit(solution)/shard_map/all_gather | solution.py:341
  27.7 28.6 %gather_fusion.1 = bf16[4224,1024]{1,0:T(8,128)(2,1)} fusion(bf16[9504,1024]{1,0:T(8,128)(2,1)} %param.17, s32[5120]{0:T(1024)S(1)} %pad_clamp_fusion.2), kind=kCustom, calls=%fused_computation.1 | custom fusion | bytes 17318400 | tf_op jit(solution)/shard_map/jit(_take)/gather | solution.py:360
  57.0 28.6 %gather_fusion = bf16[4224,1024]{1,0:T(8,128)(2,1)} fusion(bf16[9504,1024]{1,0:T(8,128)(2,1)} %param.17, s32[5120]{0:T(1024)S(1)} %pad_clamp_fusion.3), kind=kCustom, calls=%fused_computation | custom fusion | bytes 17318400 | tf_op jit(solution)/shard_map/jit(_take)/gather | solution.py:360
  96.3 29.3 %gather_fusion.3 = bf16[4224,1024]{1,0:T(8,128)(2,1)} fusion(bf16[9504,1024]{1,0:T(8,128)(2,1)} %param.17, s32[5120]{0:T(1024)S(1)} %pad_clamp_fusion), kind=kCustom, calls=%fused_computation.3 | custom fusion | bytes 17318400 | tf_op jit(solution)/shard_map/jit(_take)/gather | solution.py:360
  126.1 29.1 %gather_fusion.2 = bf16[4224,1024]{1,0:T(8,128)(2,1)} fusion(bf16[9504,1024]{1,0:T(8,128)(2,1)} %param.17, s32[5120]{0:T(1024)S(1)} %pad_clamp_fusion.1), kind=kCustom, calls=%fused_computation.2 | custom fusion | bytes 17318400 | tf_op jit(solution)/shard_map/jit(_take)/gather | solution.py:360
  155.2 11.0 select_select_fusion
  176.4 142.3 %reduce-scatter.8.cloned.1.call-done = bf16[528,1024]{1,0:T(8,128)(2,1)} async-done(((bf16[4224,1024]{1,0:T(8,128)(2,1)}), bf16[528,1024]{1,0:T(8,128)(2,1)}) %reduce-scatter.8.cloned.1.call-update) | async-done | bytes 1081360 | tf_op jit(solution)/shard_map/reduce_scatter | solution.py:321
  328.2 12.1 %slice.124.w_ref = bf16[1024,6144]{1,0:T(8,128)(2,1)} slice(bf16[1024,10240]{1,0:T(8,128)(2,1)} %all-gather.10.cloned.1.call-done), slice={[0:1024], [4096:10240]} | slice | bytes 25165824 | tf_op jit(solution)/shard_map/slice | solution.py:349
  346.5 18.2 %attn_fwd.2 = (bf16[1024,2048]{1,0:T(8,128)(2,1)}, bf16[1024,1024]{1,0:T(8,128)(2,1)}, bf16[1024,1024]{1,0:T(8,128)(2,1)}) custom-call(bf16[512,4096]{1,0:T(8,128)(2,1)} %convolution_convert_fusion.1.qkv_ref, f32[1024,128]{1,0:T(8,128)} %get-tuple-element.139.cos_ref, f32[1024,128]{1,0:T(8,128)} %get-tuple-element.140.sin_ref, ...), custom_call_target="tpu_custom_call" | custom-call | flops 12000000000 | bytes 8000000 | tf_op jit(solution)/shard_map/attn_fwd/pallas_call | solution.py:96
  375.9 18.2 %attn_fwd.3 = (bf16[1024,2048]{1,0:T(8,128)(2,1)}, bf16[1024,1024]{1,0:T(8,128)(2,1)}, bf16[1024,1024]{1,0:T(8,128)(2,1)}) custom-call(bf16[512,4096]{1,0:T(8,128)(2,1)} %convolution_convert_fusion.qkv_ref, f32[1024,128]{1,0:T(8,128)} %get-tuple-element.139.cos_ref, ...), custom_call_target="tpu_custom_call", output_to_operand_aliasing={{0}: (5, {}), {1}: (6, {}), {2}: (7, {})} | custom-call | flops 12000000000 | bytes 8000000 | tf_op jit(solution)/shard_map/attn_fwd/pallas_call | solution.py:96
  404.3 22.0 %mlp_fwd.1 = (f32[1024,6144]{1,0:T(8,128)}, bf16[1024,3072]{1,0:T(8,128)(2,1)}, bf16[1536,1024]{1,0:T(8,128)(2,1)}, bf16[1536,1024]{1,0:T(8,128)(2,1)}) custom-call(s32[1]{0:T(128)} %bitcast.7.core_ref, bf16[1024,1024]{1,0:T(8,128)(2,1)} %fusion.6.x_ref, bf16[1024,6144]{1,0:T(8,128)(2,1)} %slice.124.w_ref), custom_call_target="tpu_custom_call" | custom-call | flops 16000000000 | bytes 52000000 | tf_op jit(solution)/shard_map/mlp_fwd/pallas_call | solution.py:207
  451.3 21.5 %mlp_bwd.1 = bf16[1024,6144]{1,0:T(8,128)(2,1)} custom-call(bf16[1024,1024]{1,0:T(8,128)(2,1)} %bitcast.74, bf16[3072,1024]{1,0:T(8,128)(2,1)} %all-gather.14.cloned.1.call-done.w_ref, f32[1024,6144]{1,0:T(8,128)} %get-tuple-element.77.gu_ref), custom_call_target="tpu_custom_call" | custom-call | flops 12000000000 | bytes 46000000 | tf_op jit(solution)/shard_map/mlp_bwd/pallas_call | solution.py:232
  472.8 12.9 %fusion.64 = f32[512,6144]{1,0:T(8,128)} fusion(bf16[1024,6144]{1,0:T(8,128)(2,1)} %mlp_bwd.1, bf16[1024,1024]{1,0:T(8,128)(2,1)} %fusion.56), kind=kOutput, calls=%fused_computation.83 | convolution fusion | flops 6442450944 | bytes 26214400 | tf_op jit(solution)/shard_map/dot_general | solution.py:38
  485.8 17.7 %fusion.11 = (f32[1024]{0:T(1024)}, f32[1024]{0:T(1024)S(1)}, f32[1024,1024]{1,0:T(8,128)S(1)}) fusion(bf16[1024,1024]{1,0:T(8,128)(2,1)S(1)} %copy-done.10, f32[1024]{0:T(1024)S(1)} %add_rsqrt_fusion, f32[1024]{0:T(1024)S(1)} %mul.205, bf16[1024,6144]{1,0:T(8,128)(2,1)S(1)} %copy-done, bf16[1024,6144]{1,0:T(8,128)(2,1)} %slice.124.w_ref), kind=kOutput, calls=%fused_computation.27 | convolution fusion | flops 12892239872 | bytes 31473664 | tf_op jit(solution)/shard_map/dot_general | solution.py:34
  507.2 12.9 %convolution_add_fusion = f32[512,6144]{1,0:T(8,128)} fusion(f32[512,6144]{1,0:T(8,128)} %collective-permute-done.3, bf16[1024,6144]{1,0:T(8,128)(2,1)S(1)} %copy-done, bf16[1024,1024]{1,0:T(8,128)(2,1)} %fusion.56), kind=kOutput, calls=%fused_computation.8 | convolution fusion | flops 6445596672 | bytes 38797312 | tf_op jit(solution)/shard_map/dot_general | solution.py:38
  531.6 33.8 %attn_bwd.2 = (bf16[1024,4096]{1,0:T(8,128)(2,1)}, f32[8,128]{1,0:T(8,128)}, f32[8,128]{1,0:T(8,128)}) custom-call(bf16[512,4096]{1,0:T(8,128)(2,1)} %convolution_convert_fusion.1.qkv_ref, bf16[1024,2048]{1,0:T(8,128)(2,1)} %convolution_convert_fusion.2.do_ref, f32[1024,128]{1,0:T(8,128)} %get-tuple-element.139.cos_ref, ...), custom_call_target="tpu_custom_call" | custom-call | flops 24999999488 | bytes 14000000 | tf_op jit(solution)/shard_map/attn_bwd/pallas_call | solution.py:166
  576.2 33.6 %attn_bwd.3 = (bf16[1024,4096]{1,0:T(8,128)(2,1)}, f32[8,128]{1,0:T(8,128)}, f32[8,128]{1,0:T(8,128)}) custom-call(bf16[512,4096]{1,0:T(8,128)(2,1)} %convolution_convert_fusion.qkv_ref, bf16[1024,2048]{1,0:T(8,128)(2,1)} %convolution_convert_fusion.2.do_ref, f32[1024,128]{1,0:T(8,128)} %get-tuple-element.139.cos_ref, ...), custom_call_target="tpu_custom_call", output_to_operand_aliasing={{0}: (6, {})} | custom-call | flops 24999999488 | bytes 14000000 | tf_op jit(solution)/shard_map/attn_bwd/pallas_call | solution.py:166
  636.3 13.9 %collective-permute-done.5 = f32[1024,1024]{1,0:T(8,128)S(1)} collective-permute-done((f32[1024,1024]{1,0:T(8,128)S(1)}, f32[1024,1024]{1,0:T(8,128)S(1)}, u32[]{:S(2)}, u32[]{:S(2)}) %collective-permute-start.5) | collective-permute-done | bytes 4194336 | tf_op jit(solution)/shard_map/ppermute | solution.py:324
  663.7 11.3 %pack_tail.1 = f32[3072,1024]{1,0:T(8,128)} custom-call(f32[512,4096]{1,0:T(8,128)} %convolution_add_fusion.1.qkv_ref, f32[1024,1024]{1,0:T(8,128)} %fusion.53.out_rows_ref), custom_call_target="tpu_custom_call" | custom-call | flops 8000000000 | bytes 25000000 | tf_op jit(solution)/shard_map/pack_tail/pallas_call | solution.py:295
  677.5 12.4 %fusion.13 = bf16[1024,1024]{1,0:T(8,128)(2,1)} fusion(bf16[1024,1024]{1,0:T(8,128)(2,1)S(1)} %copy-done.11, bf16[1024,3072]{1,0:T(8,128)(2,1)} %get-tuple-element.88, bf16[3072,1024]{1,0:T(8,128)(2,1)} %all-gather.14.cloned.1.call-done.w_ref), kind=kOutput, calls=%fused_computation.29 | convolution fusion | flops 6445596672 | bytes 16777216 | tf_op jit(solution)/shard_map/dot_general | solution.py:30
  690.1 13.3 %all-gather.3 = f32[16,1,2304]{2,1,0:T(1,128)S(1)} all-gather(f32[1,1,2304]{2,1,0:T(1,128)S(1)} %reshape.438), channel_id=3, replica_groups=mesh['fsdp'=16] {'fsdp'}, dimensions={0}, use_global_device_ids=true | all-gather | bytes 156672 | tf_op jit(solution)/shard_map/all_gather | solution.py:462
  707.9 213.1 %reduce-scatter.10.cloned.1.call-done = f32[384,1024]{1,0:T(8,128)} async-done(((f32[3072,1024]{1,0:T(8,128)}), f32[384,1024]{1,0:T(8,128)}) %reduce-scatter.10.cloned.1.call-update) | async-done | bytes 1572880 | tf_op jit(solution)/shard_map/reduce_scatter | solution.py:321
  925.8 87.8 %scatter_custom_fusion = f32[9504,1024]{1,0:T(8,128)} fusion(s32[8192]{0:T(1024)S(1)} %bitcast.84, f32[8192,1024]{1,0:T(8,128)} %all-gather.16.cloned.1.call-done, f32[]{:T(128)} %constant.65.clone.1), kind=kCustom, calls=%fused_computation.6 | custom fusion | flops 8388608 | bytes 38928896 | tf_op jit(solution)/shard_map/scatter-add | solution.py:470
  1013.7 97.4 %scatter_fusion = f32[9504,1024]{1,0:T(8,128)} fusion(f32[9504,1024]{1,0:T(8,128)} %scatter_custom_fusion, s32[8192]{0:T(1024)S(1)} %bitcast.81, f32[8192,1024]{1,0:T(8,128)} %all-gather.18.cloned.1.call-done), kind=kCustom, calls=%fused_computation.5 | custom fusion | flops 8388608 | bytes 100696064 | tf_op jit(solution)/shard_map/scatter-add | solution.py:470
  (216 shorter events, 166.3 us)
Async XLA Ops:
  8.0 165.0 %reduce-scatter.6.cloned.1.call-start = ((), (), s32[]{:S(2)}) async-start(), calls=%async_computation.5 | async-start | bytes 9732096 | tf_op jit(solution)/shard_map/reduce_scatter | solution.py:321
  27.5 68.6 %copy-start.17 = (s32[8,2,2,512]{3,2,1,0:T(2,128)}, s32[8,2,2,512]{3,2,1,0:T(2,128)S(1)}, u32[]{:S(2)}) copy-start(s32[8,2,2,512]{3,2,1,0:T(2,128)S(1)} %reshape.367) | copy-start | bytes 196612
  56.3 29.3 %collective-permute-start = (bf16[4224,1024]{1,0:T(8,128)(2,1)}, bf16[4224,1024]{1,0:T(8,128)(2,1)}, u32[]{:S(2)}, u32[]{:S(2)}) collective-permute-start(bf16[4224,1024]{1,0:T(8,128)(2,1)} %gather_fusion.1), channel_id=1, source_target_pairs={{0,1},{1,0},{2,3},{3,2},{4,5},{5,4},{6,7},{7,6},{8,9},{9,8},{10,11... | collective-permute-start | bytes 25952264 | tf_op jit(solution)/shard_map/ppermute | solution.py:324
  95.9 222.8 %reduce-scatter.8.cloned.1.call-start = ((), (), s32[]{:S(2)}) async-start(), calls=%async_computation.7 | async-start | bytes 9732096 | tf_op jit(solution)/shard_map/reduce_scatter | solution.py:321
  125.7 29.6 %collective-permute-start.1 = (bf16[4224,1024]{1,0:T(8,128)(2,1)}, bf16[4224,1024]{1,0:T(8,128)(2,1)}, u32[]{:S(2)}, u32[]{:S(2)}) collective-permute-start(bf16[4224,1024]{1,0:T(8,128)(2,1)} %gather_fusion.3), channel_id=1, source_target_pairs={{0,1},{1,0},{2,3},{3,2},{4,5},{5,4},{6,7},{7,6},{8,9},{9,8},{10,11... | collective-permute-start | bytes 25952264 | tf_op jit(solution)/shard_map/ppermute | solution.py:324
  166.3 153.8 %all-gather.10.cloned.1.call-start = ((), (), s32[]{:S(2)}) async-start(), calls=%async_computation.6 | async-start | bytes 22282240 | tf_op jit(solution)/shard_map/all_gather | solution.py:318
  166.9 227.2 %all-gather.12.cloned.1.call-start = ((), (), s32[]{:S(2)}) async-start(), calls=%async_computation.8 | async-start | bytes 4456448 | tf_op jit(solution)/shard_map/all_gather | solution.py:318
  167.5 283.8 %all-gather.14.cloned.1.call-start = ((), (), s32[]{:S(2)}) async-start(), calls=%async_computation.9 | async-start | bytes 6684672 | tf_op jit(solution)/shard_map/all_gather | solution.py:318
  167.8 197.2 %copy-start.19 = (f32[1024]{0:T(1024)}, f32[1024]{0:T(1024)S(1)}, u32[]{:S(2)}) copy-start(f32[1024]{0:T(1024)S(1)} %mul.189) | copy-start | bytes 12292
  171.6 533.7 %reduce-scatter.12.cloned.1.call-start = ((), (), s32[]{:S(2)}) async-start(), calls=%async_computation.13 | async-start | bytes 14155776 | tf_op jit(solution)/shard_map/reduce_scatter | solution.py:321
  174.7 153.6 %copy-start.21 = (f32[512]{0:T(512)}, f32[512]{0:T(512)S(1)}, u32[]{:S(2)}) copy-start(f32[512]{0:T(512)S(1)} %add_rsqrt_fusion.2) | copy-start | bytes 6148
  176.4 163.9 %copy-start.14 = (bf16[512,1024]{1,0:T(8,128)(2,1)}, bf16[512,1024]{1,0:T(8,128)(2,1)S(1)}, u32[]{:S(2)}) copy-start(bf16[512,1024]{1,0:T(8,128)(2,1)S(1)} %fusion.28) | copy-start | bytes 3145732
  320.0 74.1 %copy-start.1 = (bf16[512,1024]{1,0:T(8,128)(2,1)}, bf16[512,1024]{1,0:T(8,128)(2,1)S(1)}, u32[]{:S(2)}) copy-start(bf16[512,1024]{1,0:T(8,128)(2,1)S(1)} %slice.126) | copy-start | bytes 3145732
  433.5 10.5 collective-permute-start.2
  485.7 21.5 %collective-permute-start.3 = (f32[512,6144]{1,0:T(8,128)}, f32[512,6144]{1,0:T(8,128)}, u32[]{:S(2)}, u32[]{:S(2)}) collective-permute-start(f32[512,6144]{1,0:T(8,128)} %fusion.64), channel_id=1, source_target_pairs={{0,1},{1,0},{2,3},{3,2},{4,5},{5,4},{6,7},{7,6},{8,9},{9,8},{10,11... | collective-permute-start | bytes 37748744 | tf_op jit(solution)/shard_map/ppermute | solution.py:324
  520.1 400.9 %reduce-scatter.10.cloned.1.call-start = ((), (), s32[]{:S(2)}) async-start(), calls=%async_computation.12 | async-start | bytes 14155776 | tf_op jit(solution)/shard_map/reduce_scatter | solution.py:321
  531.6 33.9 %copy-start.5 = (bf16[528,1024]{1,0:T(8,128)(2,1)S(1)}, bf16[528,1024]{1,0:T(8,128)(2,1)}, u32[]{:S(2)}) copy-start(bf16[528,1024]{1,0:T(8,128)(2,1)} %reduce-scatter.6.cloned.1.call-done) | copy-start | bytes 3244036
  531.6 33.9 %copy-start.20 = (f32[1024]{0:T(1024)S(1)}, f32[1024]{0:T(1024)}, u32[]{:S(2)}) copy-start(f32[1024]{0:T(1024)} %copy-done.19) | copy-start | bytes 12292
  531.6 33.9 %copy-start.22 = (f32[512]{0:T(512)S(1)}, f32[512]{0:T(512)}, u32[]{:S(2)}) copy-start(f32[512]{0:T(512)} %copy-done.21) | copy-start | bytes 6148
  630.8 23.8 %collective-permute-start.4 = (f32[512,4096]{1,0:T(8,128)}, f32[512,4096]{1,0:T(8,128)}, u32[]{:S(2)}, u32[]{:S(2)}) collective-permute-start(f32[512,4096]{1,0:T(8,128)} %fusion.60), channel_id=1, source_target_pairs={{0,1},{1,0},{2,3},{3,2},{4,5},{5,4},{6,7},{7,6},{8,9},{9,8},{10,11... | collective-permute-start | bytes 25165832 | tf_op jit(solution)/shard_map/ppermute | solution.py:324
  635.8 14.4 %collective-permute-start.5 = (f32[1024,1024]{1,0:T(8,128)S(1)}, f32[1024,1024]{1,0:T(8,128)S(1)}, u32[]{:S(2)}, u32[]{:S(2)}) collective-permute-start(f32[1024,1024]{1,0:T(8,128)S(1)} %fusion.45), channel_id=1, source_target_pairs={{0,1},{1,0},{2,3},{3,2},{4,5},{5,4},{6,7},{7,6},{8,9},{9,8},{10,11... | collective-permute-start | bytes 12582920 | tf_op jit(solution)/shard_map/ppermute | solution.py:324
  675.1 250.7 %all-gather.16.cloned.1.call-start = ((), (), s32[]{:S(2)}) async-start(), calls=%async_computation.10 | async-start | bytes 35651584 | tf_op jit(solution)/shard_map/all_gather | solution.py:318
  675.9 337.8 %all-gather.18.cloned.1.call-start = ((), (), s32[]{:S(2)}) async-start(), calls=%async_computation.11 | async-start | bytes 35651584 | tf_op jit(solution)/shard_map/all_gather | solution.py:318
  676.6 434.4 %reduce-scatter.14.cloned.1.call-start = ((), (), s32[]{:S(2)}) async-start(), calls=%async_computation.14 | async-start | bytes 7077888 | tf_op jit(solution)/shard_map/reduce_scatter | solution.py:321
  (32 other events, 380.8 us)
Sparse Core Ops, SparseCore 0:
  96.0 76.9 reduce-scatter.5
  177.9 140.7 reduce-scatter.7
  520.2 102.3 reduce-scatter.11
  675.2 245.6 reduce-scatter.9
  925.3 108.2 reduce-scatter.13
Sparse Core Ops, SparseCore 1:
  169.6 99.2 all-gather.9
  271.0 40.3 all-gather.11
  313.6 42.0 all-gather.13
  678.1 155.1 all-gather.15
  835.6 147.3 all-gather.17
